TPU v7x, 32 devices: a whole 2x2x4 slice. The times are simulated.
32 devices in a mesh: dev: 32 (over z, y, x, core).
Axes of the slice: x: 2, y: 2, z: 4, core: 2. Of those that a mesh axis runs over, the one named last changes fastest.
Arguments:
- tokens: bfloat16 [24576, 768], P('dev'), may hold values from -6 to 6
- cotangent: bfloat16 [24576, 768], P('dev'), may hold values from -6 to 6
- clip_start: int32 [24576], P('dev'), may hold values from 0 to 24575, as said below
- clip_end: int32 [24576], P('dev'), may hold values from 1 to 24576, as said below
- qkv_weight: float32 [3, 768, 768], P(None, 'dev'), may hold values from -0.21875 to 0.21875
- out_weight: float32 [768, 768], P('dev'), may hold values from -4 to 4
- up_weight: float32 [768, 3072], P('dev'), may hold values from -0.21875 to 0.21875
- down_weight: float32 [3072, 768], P('dev'), may hold values from -0.109375 to 0.109375
- vectors: float32 [12, 768], P(None, 'dev'), may hold values from -1.6 to 1.6, as said below
- qkv_first: float32 [3, 768, 768], P(None, 'dev'), may hold values from -48 to 48
- out_first: float32 [768, 768], P('dev'), may hold values from -48 to 48
- up_first: float32 [768, 3072], P('dev'), may hold values from -48 to 48
- down_first: float32 [3072, 768], P('dev'), may hold values from -48 to 48
- vector_first: float32 [12, 768], P(None, 'dev'), may hold values from -48 to 48
- qkv_second: float32 [3, 768, 768], P(None, 'dev'), may hold values from 7.3728 to 73.728
- out_second: float32 [768, 768], P('dev'), may hold values from 7.3728 to 73.728
- up_second: float32 [768, 3072], P('dev'), may hold values from 7.3728 to 73.728
- down_second: float32 [3072, 768], P('dev'), may hold values from 7.3728 to 73.728
- vector_second: float32 [12, 768], P(None, 'dev'), may hold values from 7.3728 to 73.728
Outputs:
- result: bfloat16 [24576, 768], P('dev')
- grad_tokens: float32 [24576, 768], P('dev')
- qkv_update: float32 [3, 768, 768], P(None, 'dev')
- out_update: float32 [768, 768], P('dev')
- up_update: float32 [768, 3072], P('dev')
- down_update: float32 [3072, 768], P('dev')
- vector_update: float32 [12, 768], P(None, 'dev')
- qkv_first_new: float32 [3, 768, 768], P(None, 'dev')
- out_first_new: float32 [768, 768], P('dev')
- up_first_new: float32 [768, 3072], P('dev')
- down_first_new: float32 [3072, 768], P('dev')
- vector_first_new: float32 [12, 768], P(None, 'dev')
- qkv_second_new: float32 [3, 768, 768], P(None, 'dev')
- out_second_new: float32 [768, 768], P('dev')
- up_second_new: float32 [768, 3072], P('dev')
- down_second_new: float32 [3072, 768], P('dev')
- vector_second_new: float32 [12, 768], P(None, 'dev')
Inputs may be any that keep to these rules, and one draw needn't show every extreme that they name: clip_start[i] <= i < clip_start[i] + 1500; clips lie end to end and all tokens of a clip share clip_start; the first clip starts at 0 and holds 1500 tokens. clip_start[i] < clip_end[i] <= clip_start[i] + 1500, equal to it for the first clip; all tokens of a clip share clip_end; tokens of a clip at or after clip_end are padding. `vectors`: rows 0 and 5 lie near 1.
All inputs are finite; a program needn't handle non-finite values.
Results may differ from a plain program's by a relative error of at most 0.023.
Values may be sent and summed in bfloat16 or wider, within the bound.
A program may use at most 384 MiB of HBM per device.

v0:
```python
import jax
import jax.numpy as jnp
from jax import lax
from jax.sharding import PartitionSpec as P

HD = 64
CLIP = 1500
STEP = 10


beta_one = 0.9
beta_two = 0.999
learn_rate = 0.02
weight_decay = 0.1
adam_eps = 1e-08
norm_eps = 1e-05
masked_score = -1e30


def shifted(value, axis, steps):
    count = lax.axis_size(axis)
    initial, last = (max(0, -steps), min(count, count - steps))
    return lax.ppermute(value, axis, [(source, source + steps) for source in range(initial, last)])


def exact_gelu(values):
    return jax.nn.gelu(values, approximate=False)


def norm_forward(values, gain_row, bias_row):
    centre = values - jnp.mean(values, axis=-1, keepdims=True)
    inverse = lax.rsqrt(jnp.mean(centre * centre, axis=-1, keepdims=True) + norm_eps)
    unit_value = centre * inverse
    return (unit_value * gain_row + bias_row, unit_value, inverse)


def norm_backward(grad_output, unit_value, inverse, gain_row):
    grad_unit = grad_output * gain_row
    grad_input = inverse * (
        grad_unit
        - jnp.mean(grad_unit, axis=-1, keepdims=True)
        - unit_value * jnp.mean(grad_unit * unit_value, axis=-1, keepdims=True)
    )
    return (grad_input, jnp.sum(grad_output * unit_value, axis=0), jnp.sum(grad_output, axis=0))


def masked_scores(query_heads, key_heads, key_first, lower_bound, upper_bound):
    head_size = query_heads.shape[-1]
    scores = jnp.einsum(
        "qhd,khd->hqk", query_heads, key_heads, preferred_element_type=jnp.float32
    ) * head_size ** (-0.5)
    places = key_first + jnp.arange(key_heads.shape[0], dtype=jnp.int32)
    allowed = (places[None, :] >= lower_bound[:, None]) & (places[None, :] < upper_bound[:, None])
    return jnp.where(allowed[None], scores, masked_score)


def attention_grads(
    query_heads,
    grad_heads,
    log_total,
    delta,
    lower_bound,
    upper_bound,
    key_heads,
    value_heads,
    key_first,
):
    head_size = query_heads.shape[-1]
    scores = masked_scores(query_heads, key_heads, key_first, lower_bound, upper_bound)
    probs_wide = jnp.exp(scores - log_total[..., None])
    probs_low = probs_wide.astype(jnp.bfloat16)
    grad_values_part = jnp.einsum(
        "hqk,qhd->khd", probs_low, grad_heads, preferred_element_type=jnp.float32
    )
    grad_probs = jnp.einsum(
        "qhd,khd->hqk", grad_heads, value_heads, preferred_element_type=jnp.float32
    )
    grad_scores = (probs_wide * (grad_probs - delta[..., None])).astype(jnp.bfloat16)
    grad_query_part = jnp.einsum(
        "hqk,khd->qhd", grad_scores, key_heads, preferred_element_type=jnp.float32
    ) * head_size ** (-0.5)
    grad_keys_part = jnp.einsum(
        "hqk,qhd->khd", grad_scores, query_heads, preferred_element_type=jnp.float32
    ) * head_size ** (-0.5)
    return (grad_query_part, grad_keys_part, grad_values_part)


def adamw_step(master, gradient, first_moment, second_moment):
    first_new = beta_one * first_moment + (1.0 - beta_one) * gradient
    second_new = beta_two * second_moment + (1.0 - beta_two) * gradient * gradient
    fix_one = 1.0 - beta_one**STEP
    fix_two = 1.0 - beta_two**STEP
    update = -learn_rate * (
        first_new / fix_one / (jnp.sqrt(second_new / fix_two) + adam_eps) + weight_decay * master
    )
    return (update, first_new, second_new)


def per_device(
    tokens,
    cotangent,
    clip_start,
    clip_end,
    qkv_weight,
    out_weight,
    up_weight,
    down_weight,
    vectors,
    qkv_first,
    out_first,
    up_first,
    down_first,
    vector_first,
    qkv_second,
    out_second,
    up_second,
    down_second,
    vector_second,
):
    row_count = tokens.shape[0]
    device_index = lax.axis_index("dev")
    row_first = device_index * row_count
    shards = (
        qkv_weight.astype(jnp.bfloat16),
        out_weight.astype(jnp.bfloat16),
        up_weight.astype(jnp.bfloat16),
        down_weight.astype(jnp.bfloat16),
        vectors.astype(jnp.bfloat16),
    )
    qkv_full, out_full, up_full, down_full, vector_low = (
        lax.all_gather(shards[0], "dev", axis=1, tiled=True),
        lax.all_gather(shards[1], "dev", axis=0, tiled=True),
        lax.all_gather(shards[2], "dev", axis=0, tiled=True),
        lax.all_gather(shards[3], "dev", axis=0, tiled=True),
        lax.all_gather(shards[4], "dev", axis=1, tiled=True),
    )
    vector_full = vector_low.astype(jnp.float32)
    width = out_full.shape[1]
    head_count = width // HD
    hidden_width = up_full.shape[1]
    tokens_wide = tokens.astype(jnp.float32)
    normed_wide, unit_one, inverse_one = norm_forward(tokens_wide, vector_full[0], vector_full[1])
    normed = normed_wide.astype(jnp.bfloat16)
    projected = jnp.einsum("td,kde->kte", normed, qkv_full, preferred_element_type=jnp.float32)
    query = (projected[0] + vector_full[2]).astype(jnp.bfloat16)
    key_values = jnp.stack([projected[1], projected[2] + vector_full[3]]).astype(jnp.bfloat16)
    reach = (row_count + CLIP - 2) // row_count
    offsets = [offset for offset in range(-reach, reach + 1) if offset != 0]
    key_blocks = [(key_values, row_first)]
    for offset in offsets:
        arrived = shifted(key_values, "dev", offset)
        key_blocks.append((arrived, (device_index - offset) * row_count))
    query_heads = query.reshape(row_count, head_count, HD)
    peak = jnp.full((head_count, row_count), masked_score, jnp.float32)
    totals = jnp.zeros((head_count, row_count), jnp.float32)
    for kv_block, key_first in key_blocks:
        scores = masked_scores(
            query_heads,
            kv_block[0].reshape(row_count, head_count, HD),
            key_first,
            clip_start,
            clip_end,
        )
        new_peak = jnp.maximum(peak, jnp.max(scores, axis=-1))
        totals = totals * jnp.exp(peak - new_peak) + jnp.sum(
            jnp.exp(scores - new_peak[..., None]), axis=-1
        )
        peak = new_peak
    log_total = peak + jnp.log(totals)
    mixed_wide = jnp.zeros((row_count, head_count, HD), jnp.float32)
    for kv_block, key_first in key_blocks:
        scores = masked_scores(
            query_heads,
            kv_block[0].reshape(row_count, head_count, HD),
            key_first,
            clip_start,
            clip_end,
        )
        weights = jnp.exp(scores - log_total[..., None]).astype(jnp.bfloat16)
        mixed_wide = mixed_wide + jnp.einsum(
            "hqk,khd->qhd",
            weights,
            kv_block[1].reshape(row_count, head_count, HD),
            preferred_element_type=jnp.float32,
        )
    mixed = mixed_wide.reshape(row_count, width).astype(jnp.bfloat16)
    branch = jnp.dot(mixed, out_full, preferred_element_type=jnp.float32) + vector_full[4]
    middle = tokens_wide + branch
    normed_two_wide, unit_two, inverse_two = norm_forward(middle, vector_full[5], vector_full[6])
    normed_two = normed_two_wide.astype(jnp.bfloat16)
    up_bias = vector_full[8:].reshape(hidden_width)
    hidden = jnp.dot(normed_two, up_full, preferred_element_type=jnp.float32) + up_bias
    active = exact_gelu(hidden).astype(jnp.bfloat16)
    result = (
        middle + jnp.dot(active, down_full, preferred_element_type=jnp.float32) + vector_full[7]
    ).astype(jnp.bfloat16)
    qkv_back, out_back, up_back, down_back, vector_again_low = (
        lax.all_gather(shards[0], "dev", axis=1, tiled=True),
        lax.all_gather(shards[1], "dev", axis=0, tiled=True),
        lax.all_gather(shards[2], "dev", axis=0, tiled=True),
        lax.all_gather(shards[3], "dev", axis=0, tiled=True),
        lax.all_gather(shards[4], "dev", axis=1, tiled=True),
    )
    vector_again = vector_again_low.astype(jnp.float32)
    grad_output = cotangent.astype(jnp.float32)
    grad_down = jnp.einsum("tf,td->fd", active, cotangent, preferred_element_type=jnp.float32)
    grad_active = jnp.einsum("td,fd->tf", cotangent, down_back, preferred_element_type=jnp.float32)
    gelu_pull = jax.vjp(exact_gelu, hidden)[1]
    grad_hidden = gelu_pull(grad_active)[0].astype(jnp.bfloat16)
    grad_up = jnp.einsum("td,tf->df", normed_two, grad_hidden, preferred_element_type=jnp.float32)
    grad_up_bias = jnp.sum(grad_hidden.astype(jnp.float32), axis=0)
    grad_normed_two = jnp.einsum(
        "tf,df->td", grad_hidden, up_back, preferred_element_type=jnp.float32
    )
    grad_from_two, grad_gain_two, grad_bias_two = norm_backward(
        grad_normed_two, unit_two, inverse_two, vector_again[5]
    )
    grad_middle = grad_output + grad_from_two
    grad_branch = grad_middle.astype(jnp.bfloat16)
    grad_out_weight = jnp.einsum(
        "td,te->de", mixed, grad_branch, preferred_element_type=jnp.float32
    )
    grad_out_bias = jnp.sum(grad_branch.astype(jnp.float32), axis=0)
    grad_mixed = jnp.einsum(
        "te,de->td", grad_branch, out_back, preferred_element_type=jnp.float32
    ).astype(jnp.bfloat16)
    grad_heads = grad_mixed.reshape(row_count, head_count, HD)
    delta = jnp.sum(
        grad_heads.astype(jnp.float32)
        * mixed.reshape(row_count, head_count, HD).astype(jnp.float32),
        axis=-1,
    ).T
    grad_query_wide = jnp.zeros((row_count, head_count, HD), jnp.float32)
    returned = jnp.zeros((2, row_count, width), jnp.float32)
    for position, (kv_block, key_first) in enumerate(key_blocks):
        key_heads = kv_block[0].reshape(row_count, head_count, HD)
        value_heads = kv_block[1].reshape(row_count, head_count, HD)
        query_part, keys_part, values_part = attention_grads(
            query_heads,
            grad_heads,
            log_total,
            delta,
            clip_start,
            clip_end,
            key_heads,
            value_heads,
            key_first,
        )
        grad_query_wide = grad_query_wide + query_part
        pair = jnp.stack(
            [keys_part.reshape(row_count, width), values_part.reshape(row_count, width)]
        )
        if position == 0:
            returned = pair
        else:
            returned = returned + shifted(
                pair.astype(jnp.bfloat16), "dev", -offsets[position - 1]
            ).astype(pair.dtype)
    grad_kv = returned.astype(jnp.bfloat16)
    grad_query = grad_query_wide.reshape(row_count, width).astype(jnp.bfloat16)
    grad_project = jnp.stack([grad_query, grad_kv[0], grad_kv[1]])
    grad_qkv = jnp.einsum("td,kte->kde", normed, grad_project, preferred_element_type=jnp.float32)
    grad_normed = jnp.einsum(
        "kte,kde->td", grad_project, qkv_back, preferred_element_type=jnp.float32
    )
    grad_from_one, grad_gain_one, grad_bias_one = norm_backward(
        grad_normed, unit_one, inverse_one, vector_again[0]
    )
    grad_tokens = grad_middle + grad_from_one
    grad_vectors = jnp.concatenate(
        [
            jnp.stack(
                [
                    grad_gain_one,
                    grad_bias_one,
                    jnp.sum(grad_query.astype(jnp.float32), axis=0),
                    jnp.sum(grad_kv[1].astype(jnp.float32), axis=0),
                    grad_out_bias,
                    grad_gain_two,
                    grad_bias_two,
                    jnp.sum(grad_output, axis=0),
                ]
            ),
            grad_up_bias.reshape(-1, width),
        ],
        axis=0,
    )
    owned = (
        lax.psum_scatter(grad_qkv, "dev", scatter_dimension=1, tiled=True),
        lax.psum_scatter(grad_out_weight, "dev", scatter_dimension=0, tiled=True),
        lax.psum_scatter(grad_up, "dev", scatter_dimension=0, tiled=True),
        lax.psum_scatter(grad_down, "dev", scatter_dimension=0, tiled=True),
        lax.psum_scatter(grad_vectors, "dev", scatter_dimension=1, tiled=True),
    )
    masters = (qkv_weight, out_weight, up_weight, down_weight, vectors)
    firsts = (qkv_first, out_first, up_first, down_first, vector_first)
    seconds = (qkv_second, out_second, up_second, down_second, vector_second)
    stepped = [
        adamw_step(masters[place], owned[place], firsts[place], seconds[place])
        for place in range(5)
    ]
    return (
        result,
        grad_tokens,
        stepped[0][0],
        stepped[1][0],
        stepped[2][0],
        stepped[3][0],
        stepped[4][0],
        stepped[0][1],
        stepped[1][1],
        stepped[2][1],
        stepped[3][1],
        stepped[4][1],
        stepped[0][2],
        stepped[1][2],
        stepped[2][2],
        stepped[3][2],
        stepped[4][2],
    )


def solution(mesh):
    in_specs = (
        P("dev", None),
        P("dev", None),
        P("dev"),
        P("dev"),
        P(None, "dev", None),
        P("dev", None),
        P("dev", None),
        P("dev", None),
        P(None, "dev"),
        P(None, "dev", None),
        P("dev", None),
        P("dev", None),
        P("dev", None),
        P(None, "dev"),
        P(None, "dev", None),
        P("dev", None),
        P("dev", None),
        P("dev", None),
        P(None, "dev"),
    )
    out_specs = (
        P("dev", None),
        P("dev", None),
        P(None, "dev", None),
        P("dev", None),
        P("dev", None),
        P("dev", None),
        P(None, "dev"),
        P(None, "dev", None),
        P("dev", None),
        P("dev", None),
        P("dev", None),
        P(None, "dev"),
        P(None, "dev", None),
        P("dev", None),
        P("dev", None),
        P("dev", None),
        P(None, "dev"),
    )
    return jax.shard_map(
        per_device, mesh=mesh, in_specs=in_specs, out_specs=out_specs, check_vma=False
    )
```

profile of v0, /device:TPU:0, one launch (start us, length us, event | category | flops | bytes accessed | tf_op | source)
XLA Modules:
  0.0 1412.9 jit_solution(9992444680322382248)
XLA Ops:
  15.3 43.9 %all-gather = bf16[32,24,12]{1,2,0:T(8,128)(2,1)S(1)} all-gather(bf16[1,24,12]{1,2,0:T(8,128)(2,1)S(1)} %convert_bitcast_fusion), channel_id=1, replica_groups=mesh['dev'=32] {'dev'}, dimensions={0}, use_global_device_ids=true | all-gather | bytes 19008 | tf_op jit(solution)/shard_map/all_gather | solution.py:135
  112.1 26.6 %collective-permute-done = bf16[2,768,768]{1,2,0:T(8,128)(2,1)} collective-permute-done((bf16[2,768,768]{1,2,0:T(8,128)(2,1)}, bf16[2,768,768]{1,2,0:T(8,128)(2,1)}, u32[]{:S(2)}, u32[]{:S(2)}) %collective-permute-start) | collective-permute-done | bytes 2359328 | tf_op jit(solution)/shard_map/ppermute | solution.py:23
  175.7 42.8 %collective-permute-done.3 = bf16[2,768,768]{1,2,0:T(8,128)(2,1)S(1)} collective-permute-done((bf16[2,768,768]{1,2,0:T(8,128)(2,1)}, bf16[2,768,768]{1,2,0:T(8,128)(2,1)S(1)}, u32[]{:S(2)}, u32[]{:S(2)}) %collective-permute-start.3) | collective-permute-done | bytes 2359328 | tf_op jit(solution)/shard_map/ppermute | solution.py:23
  244.3 21.7 %exponential_reduce_fusion = (f32[12,768]{1,0:T(8,128)S(1)}, f32[12,768]{1,0:T(8,128)S(1)}) fusion(f32[12,768,768]{1,2,0:T(8,128)} %get-tuple-element.143, f32[12,768]{1,0:T(8,128)S(1)} %get-tuple-element.121, pred[768,768]{0,1:T(8,128)(4,1)S(1)} %get-tuple-element.141, f32[12,768]{1,0:T(8,128)S(1)} %get-tuple-element.122, ...), kind=kLoop, calls=%fused_computation.10 | loop fusion | flops 56604672 | bytes 57950208 | tf_op jit(solution)/shard_map/reduce_sum | solution.py:165
  266.0 21.6 %exponential_reduce_fusion.2 = (f32[12,768]{1,0:T(8,128)S(1)}, f32[12,768]{1,0:T(8,128)S(1)}) fusion(f32[12,768,768]{1,2,0:T(8,128)} %get-tuple-element.147, f32[12,768]{1,0:T(8,128)S(1)} %get-tuple-element.123, pred[768,768]{0,1:T(8,128)(4,1)S(1)} %get-tuple-element.139, f32[12,768]{1,0:T(8,128)S(1)} %get-tuple-element.124, ...), kind=kLoop, calls=%fused_computation.12 | loop fusion | flops 56604672 | bytes 57950208 | tf_op jit(solution)/shard_map/reduce_sum | solution.py:165
  315.4 14.8 %fusion.50 = f32[12,64,768]{2,1,0:T(8,128)} fusion(bf16[768,12,64]{0,2,1:T(8,128)(2,1)S(1)} %bitcast.178, f32[12,768,768]{1,2,0:T(8,128)} %get-tuple-element.145, f32[12,768]{1,0:T(8,128)S(1)} %log_add_fusion, pred[768,768]{0,1:T(8,128)(4,1)S(1)} %get-tuple-element.140), kind=kOutput, calls=%fused_computation.133 | convolution fusion | flops 934281216 | bytes 32477184 | tf_op jit(solution)/shard_map/hqk,khd->qhd/dot_general | solution.py:180
  330.2 14.0 fusion.60
  344.3 16.9 %add_convert_fusion.3 = bf16[12,64,768]{2,1,0:T(8,128)(2,1)} fusion(f32[12,64,768]{2,1,0:T(8,128)} %fusion.50, f32[12,64,768]{2,1,0:T(8,128)} %fusion.53, f32[12,64,768]{2,1,0:T(8,128)} %fusion.60, f32[12,64,768]{2,1,0:T(8,128)} %fusion.56, bf16[768,12,64]{0,2,1:T(8,128)(2,1)S(1)} %bitcast.180, f32[12,768,768]{1,2,0:T(8,128)} %get-tuple-element.143, ...), kind=kOutput, calls=%fused_computation.97 | convolution fusion | flops 937230336 | bytes 40734720 | tf_op jit(solution)/shard_map/hqk,khd->qhd/dot_general | solution.py:180
  373.9 29.8 %convert_reduce_fusion = (f32[3072]{0:T(1024)}, bf16[768,3072]{1,0:T(8,128)(2,1)S(1)}, f32[768,3072]{1,0:T(8,128)}) fusion(f32[768,3072]{1,0:T(8,128)} %fusion.90, f32[3072]{0:T(1024)} %add.392, bf16[768,768]{1,0:T(8,128)(2,1)S(1)} %copy-done.49, bf16[3072,768]{1,0:T(8,128)(2,1)} %all-gather.12.cloned.1.call-done), kind=kOutput, calls=%fused_computation.32 | convolution fusion | flops 3800822784 | bytes 29515776 | tf_op jit(solution)/shard_map/td,fd->tf/dot_general | solution.py:207
  420.4 14.1 %convolution_convert_fusion.1 = bf16[12,64,768]{2,1,0:T(8,128)(2,1)} fusion(bf16[768,12,64]{0,2,1:T(8,128)(2,1)S(1)} %bitcast.161, f32[12,768,768]{1,2,0:T(8,128)} %get-tuple-element.143, f32[12,768]{1,0:T(8,128)S(1)} %copy-done.85, pred[768,768]{0,1:T(8,128)(4,1)S(1)} %copy-done.30), kind=kOutput, calls=%fused_computation.111 | convolution fusion | flops 934871040 | bytes 31297536 | tf_op jit(solution)/shard_map/hqk,qhd->khd/dot_general | solution.py:72
  448.6 19.1 %multiply_convert_fusion = bf16[12,768,768]{1,2,0:T(8,128)(2,1)} fusion(f32[12,768,768]{1,2,0:T(8,128)} %get-tuple-element.143, f32[12,768]{1,0:T(8,128)S(1)} %bitcast.184, f32[12,768]{1,0:T(8,128)S(1)} %copy-done.85, pred[768,768]{0,1:T(8,128)(4,1)S(1)} %copy-done.30, bf16[768,12,64]{0,2,1:T(8,128)(2,1)S(1)} %bitcast.163, bf16[768,12,64]{0,2,1:T(8,128)(2,1)S(1)} %bitcast.181), kind=kOutput, calls=%fused_computation | convolution fusion | flops 948436992 | bytes 45490176 | tf_op jit(solution)/shard_map/qhd,khd->hqk/dot_general | solution.py:75
  467.7 19.3 %multiply_convert_fusion.1 = bf16[12,768,768]{1,2,0:T(8,128)(2,1)} fusion(f32[12,768,768]{1,2,0:T(8,128)} %get-tuple-element.145, f32[12,768]{1,0:T(8,128)S(1)} %bitcast.185, f32[12,768]{1,0:T(8,128)S(1)} %copy-done.85, pred[768,768]{0,1:T(8,128)(4,1)S(1)} %copy-done.28, bf16[768,12,64]{0,2,1:T(8,128)(2,1)S(1)} %bitcast.164, ...), kind=kOutput, calls=%fused_computation.1 | convolution fusion | flops 948436992 | bytes 45490176 | tf_op jit(solution)/shard_map/qhd,khd->hqk/dot_general | solution.py:75
  519.6 19.7 %multiply_convert_fusion.2 = bf16[12,768,768]{1,2,0:T(8,128)(2,1)} fusion(f32[12,768,768]{1,2,0:T(8,128)} %get-tuple-element.147, f32[12,768]{1,0:T(8,128)S(1)} %bitcast.186, f32[12,768]{1,0:T(8,128)S(1)} %copy-done.85, pred[768,768]{0,1:T(8,128)(4,1)S(1)} %copy-done.26, bf16[768,12,64]{0,2,1:T(8,128)(2,1)S(1)} %bitcast.166, ...), kind=kOutput, calls=%fused_computation.2 | convolution fusion | flops 948436992 | bytes 45490176 | tf_op jit(solution)/shard_map/qhd,khd->hqk/dot_general | solution.py:75
  557.9 14.0 convolution_convert_fusion.4
  571.9 19.3 %multiply_convert_fusion.3 = bf16[12,768,768]{1,2,0:T(8,128)(2,1)} fusion(f32[12,768,768]{1,2,0:T(8,128)} %get-tuple-element.149, f32[12,768]{1,0:T(8,128)S(1)} %bitcast.187, f32[12,768]{1,0:T(8,128)S(1)} %copy-done.86, pred[768,768]{0,1:T(8,128)(4,1)S(1)} %copy-done.24, bf16[768,12,64]{0,2,1:T(8,128)(2,1)S(1)} %bitcast.168, ...), kind=kOutput, calls=%fused_computation.3 | convolution fusion | flops 948436992 | bytes 45490176 | tf_op jit(solution)/shard_map/qhd,khd->hqk/dot_general | solution.py:75
  610.8 14.3 %fusion.58 = f32[12,64,768]{2,1,0:T(8,128)} fusion(bf16[768,12,64]{0,2,1:T(8,128)(2,1)S(1)} %bitcast.169, f32[12,768,768]{1,2,0:T(8,128)} %get-tuple-element.151, f32[12,768]{1,0:T(8,128)S(1)} %copy-done.86, pred[768,768]{0,1:T(8,128)(4,1)S(1)} %copy-done.22), kind=kOutput, calls=%fused_computation.136 | convolution fusion | flops 934281216 | bytes 32477184 | tf_op jit(solution)/shard_map/hqk,qhd->khd/dot_general | solution.py:72
  625.1 19.3 %multiply_convert_fusion.4 = bf16[12,768,768]{1,2,0:T(8,128)(2,1)} fusion(f32[12,768,768]{1,2,0:T(8,128)} %get-tuple-element.151, f32[12,768]{1,0:T(8,128)S(1)} %bitcast.188, f32[12,768]{1,0:T(8,128)S(1)} %copy-done.86, pred[768,768]{0,1:T(8,128)(4,1)S(1)} %copy-done.22, bf16[768,12,64]{0,2,1:T(8,128)(2,1)S(1)} %bitcast.170, ...), kind=kOutput, calls=%fused_computation.4 | convolution fusion | flops 948436992 | bytes 45490176 | tf_op jit(solution)/shard_map/qhd,khd->hqk/dot_general | solution.py:75
  684.2 58.8 %collective-permute-start.4 = (bf16[2,768,768]{2,1,0:T(8,128)(2,1)}, bf16[2,768,768]{2,1,0:T(8,128)(2,1)}, u32[]{:S(2)}, u32[]{:S(2)}) collective-permute-start(bf16[2,768,768]{2,1,0:T(8,128)(2,1)} %pad_maximum_fusion.2), channel_id=1, source_target_pairs={{0,2},{1,3},{2,4},{3,5},{4,6},{5,7},{6,8},{7,9},{8,10},{9,11},{10,... | collective-permute-start | bytes 7077896 | tf_op jit(solution)/shard_map/ppermute | solution.py:23
  781.9 92.6 %collective-permute-done.4 = bf16[2,768,768]{2,1,0:T(8,128)(2,1)} collective-permute-done((bf16[2,768,768]{2,1,0:T(8,128)(2,1)}, bf16[2,768,768]{2,1,0:T(8,128)(2,1)}, u32[]{:S(2)}, u32[]{:S(2)}) %collective-permute-start.4) | collective-permute-done | bytes 2359328 | tf_op jit(solution)/shard_map/ppermute | solution.py:23
  874.5 24.1 %collective-permute-done.7 = bf16[2,768,768]{2,1,0:T(8,128)(2,1)} collective-permute-done((bf16[2,768,768]{2,1,0:T(8,128)(2,1)}, bf16[2,768,768]{2,1,0:T(8,128)(2,1)}, u32[]{:S(2)}, u32[]{:S(2)}) %collective-permute-start.7) | collective-permute-done | bytes 2359328 | tf_op jit(solution)/shard_map/ppermute | solution.py:23
  993.0 40.2 %all-reduce.1 = f32[12,768]{1,0:T(8,128)S(1)} all-reduce(f32[12,768]{1,0:T(8,128)S(1)} %concatenate.3), channel_id=6, replica_groups=mesh['dev'=32] {'dev'}, use_global_device_ids=true, to_apply=%region_32.33.clone | all-reduce | flops 9216 | bytes 73728
  1035.6 85.0 %all-reduce.4.cloned.1.call-done = f32[3,768,768]{2,0,1:T(4,128)} async-done(((f32[3,768,768]{2,0,1:T(4,128)}), f32[3,768,768]{2,0,1:T(4,128)}) %all-reduce.4.cloned.1.call-update) | async-done | bytes 7077904
  1122.6 140.2 %reduce-scatter.7.cloned.1.call-done = f32[24,3072]{1,0:T(8,128)} async-done(((f32[768,3072]{1,0:T(8,128)}), f32[24,3072]{1,0:T(8,128)}) %reduce-scatter.7.cloned.1.call-update) | async-done | bytes 294928 | tf_op jit(solution)/shard_map/reduce_scatter | solution.py:291
  1264.8 139.1 %reduce-scatter.9.cloned.1.call-done = f32[96,768]{1,0:T(8,128)} async-done(((f32[3072,768]{1,0:T(8,128)}), f32[96,768]{1,0:T(8,128)}) %reduce-scatter.9.cloned.1.call-update) | async-done | bytes 294928 | tf_op jit(solution)/shard_map/reduce_scatter | solution.py:292
  (376 shorter events, 446.1 us)
Async XLA Ops:
  7.2 67.3 %all-gather.6.cloned.1.call-start = ((), (), s32[]{:S(2)}) async-start(), calls=%async_computation.3 | async-start | bytes 3649536 | tf_op jit(solution)/shard_map/all_gather | solution.py:131
  8.9 352.2 %all-gather.8.cloned.1.call-start = ((), (), s32[]{:S(2)}) async-start(), calls=%async_computation.4 | async-start | bytes 1216512 | tf_op jit(solution)/shard_map/all_gather | solution.py:132
  10.5 353.9 %all-gather.10.cloned.1.call-start = ((), (), s32[]{:S(2)}) async-start(), calls=%async_computation.5 | async-start | bytes 4866048 | tf_op jit(solution)/shard_map/all_gather | solution.py:133
  12.2 361.6 %all-gather.12.cloned.1.call-start = ((), (), s32[]{:S(2)}) async-start(), calls=%async_computation.6 | async-start | bytes 4866048 | tf_op jit(solution)/shard_map/all_gather | solution.py:134
  14.0 1020.0 %reduce-scatter.5.cloned.1.call-start = ((), (), s32[]{:S(2)}) async-start(), calls=%async_computation.7 | async-start | bytes 2433024 | tf_op jit(solution)/shard_map/reduce_scatter | solution.py:290
  82.1 56.6 %collective-permute-start = (bf16[2,768,768]{1,2,0:T(8,128)(2,1)}, bf16[2,768,768]{1,2,0:T(8,128)(2,1)}, u32[]{:S(2)}, u32[]{:S(2)}) collective-permute-start(bf16[2,768,768]{1,2,0:T(8,128)(2,1)} %pad_maximum_fusion.1), channel_id=1, source_target_pairs={{2,0},{3,1},{4,2},{5,3},{6,4},{7,5},{8,6},{9,7},{10,8},{11,9},{12,... | collective-permute-start | bytes 7077896 | tf_op jit(solution)/shard_map/ppermute | solution.py:23
  92.0 238.2 %copy-start.21 = (pred[768,768]{0,1:T(8,128)(4,1)}, pred[768,768]{0,1:T(8,128)(4,1)S(1)}, u32[]{:S(2)}) copy-start(pred[768,768]{0,1:T(8,128)(4,1)S(1)} %get-tuple-element.137) | copy-start | bytes 1769476
  92.0 252.3 %copy-start.29 = (pred[768,768]{0,1:T(8,128)(4,1)}, pred[768,768]{0,1:T(8,128)(4,1)S(1)}, u32[]{:S(2)}) copy-start(pred[768,768]{0,1:T(8,128)(4,1)S(1)} %get-tuple-element.141) | copy-start | bytes 1769476
  92.0 126.5 %collective-permute-start.3 = (bf16[2,768,768]{1,2,0:T(8,128)(2,1)}, bf16[2,768,768]{1,2,0:T(8,128)(2,1)S(1)}, u32[]{:S(2)}, u32[]{:S(2)}) collective-permute-start(bf16[2,768,768]{1,2,0:T(8,128)(2,1)} %pad_maximum_fusion.1), channel_id=1, source_target_pairs={{0,2},{1,3},{2,4},{3,5},{4,6},{5,7},{6,8},{7,9},{8,10},{9,11},{10,... | collective-permute-start | bytes 7077896 | tf_op jit(solution)/shard_map/ppermute | solution.py:23
  96.7 55.5 %collective-permute-start.2 = (bf16[2,768,768]{1,2,0:T(8,128)(2,1)}, bf16[2,768,768]{1,2,0:T(8,128)(2,1)S(1)}, u32[]{:S(2)}, u32[]{:S(2)}) collective-permute-start(bf16[2,768,768]{1,2,0:T(8,128)(2,1)} %pad_maximum_fusion.1), channel_id=1, source_target_pairs={{0,1},{1,2},{2,3},{3,4},{4,5},{5,6},{6,7},{7,8},{8,9},{9,10},{10,1... | collective-permute-start | bytes 7077896 | tf_op jit(solution)/shard_map/ppermute | solution.py:23
  98.4 53.9 %collective-permute-start.1 = (bf16[2,768,768]{1,2,0:T(8,128)(2,1)}, bf16[2,768,768]{1,2,0:T(8,128)(2,1)S(1)}, u32[]{:S(2)}, u32[]{:S(2)}) collective-permute-start(bf16[2,768,768]{1,2,0:T(8,128)(2,1)} %pad_maximum_fusion.1), channel_id=1, source_target_pairs={{1,0},{2,1},{3,2},{4,3},{5,4},{6,5},{7,6},{8,7},{9,8},{10,9},{11,1... | collective-permute-start | bytes 7077896 | tf_op jit(solution)/shard_map/ppermute | solution.py:23
  684.2 190.3 %collective-permute-start.4 = (bf16[2,768,768]{2,1,0:T(8,128)(2,1)}, bf16[2,768,768]{2,1,0:T(8,128)(2,1)}, u32[]{:S(2)}, u32[]{:S(2)}) collective-permute-start(bf16[2,768,768]{2,1,0:T(8,128)(2,1)} %pad_maximum_fusion.2), channel_id=1, source_target_pairs={{0,2},{1,3},{2,4},{3,5},{4,6},{5,7},{6,8},{7,9},{8,10},{9,11},{10,... | collective-permute-start | bytes 7077896 | tf_op jit(solution)/shard_map/ppermute | solution.py:23
  744.7 129.8 %collective-permute-start.5 = (bf16[2,768,768]{2,1,0:T(8,128)(2,1)}, bf16[2,768,768]{2,1,0:T(8,128)(2,1)}, u32[]{:S(2)}, u32[]{:S(2)}) collective-permute-start(bf16[2,768,768]{2,1,0:T(8,128)(2,1)} %pad_maximum_fusion.3), channel_id=1, source_target_pairs={{0,1},{1,2},{2,3},{3,4},{4,5},{5,6},{6,7},{7,8},{8,9},{9,10},{10,1... | collective-permute-start | bytes 7077896 | tf_op jit(solution)/shard_map/ppermute | solution.py:23
  749.2 125.2 %collective-permute-start.6 = (bf16[2,768,768]{2,1,0:T(8,128)(2,1)}, bf16[2,768,768]{2,1,0:T(8,128)(2,1)}, u32[]{:S(2)}, u32[]{:S(2)}) collective-permute-start(bf16[2,768,768]{2,1,0:T(8,128)(2,1)} %pad_maximum_fusion.4), channel_id=1, source_target_pairs={{1,0},{2,1},{3,2},{4,3},{5,4},{6,5},{7,6},{8,7},{9,8},{10,9},{11,1... | collective-permute-start | bytes 7077896 | tf_op jit(solution)/shard_map/ppermute | solution.py:23
  752.4 146.1 %collective-permute-start.7 = (bf16[2,768,768]{2,1,0:T(8,128)(2,1)}, bf16[2,768,768]{2,1,0:T(8,128)(2,1)}, u32[]{:S(2)}, u32[]{:S(2)}) collective-permute-start(bf16[2,768,768]{2,1,0:T(8,128)(2,1)} %pad_maximum_fusion.5), channel_id=1, source_target_pairs={{2,0},{3,1},{4,2},{5,3},{6,4},{7,5},{8,6},{9,7},{10,8},{11,9},{12,... | collective-permute-start | bytes 7077896 | tf_op jit(solution)/shard_map/ppermute | solution.py:23
  756.3 364.3 %all-reduce.4.cloned.1.call-start = ((), (), s32[]{:S(2)}) async-start(), calls=%async_computation.10 | async-start | bytes 18874368
  923.0 339.7 %reduce-scatter.7.cloned.1.call-start = ((), (), s32[]{:S(2)}) async-start(), calls=%async_computation.8 | async-start | bytes 9732096 | tf_op jit(solution)/shard_map/reduce_scatter | solution.py:291
  933.5 470.3 %reduce-scatter.9.cloned.1.call-start = ((), (), s32[]{:S(2)}) async-start(), calls=%async_computation.9 | async-start | bytes 9732096 | tf_op jit(solution)/shard_map/reduce_scatter | solution.py:292
  992.9 269.9 %copy-start.51 = (f32[24,3072]{1,0:T(8,128)S(1)}, f32[24,3072]{1,0:T(8,128)}, u32[]{:S(2)}) copy-start(f32[24,3072]{1,0:T(8,128)} %param.25) | copy-start | bytes 884740
  992.9 269.9 %copy-start.69 = (f32[24,3072]{1,0:T(8,128)S(1)}, f32[24,3072]{1,0:T(8,128)}, u32[]{:S(2)}) copy-start(f32[24,3072]{1,0:T(8,128)} %param.30) | copy-start | bytes 884740
  992.9 269.9 %copy-start.70 = (f32[24,3072]{1,0:T(8,128)S(1)}, f32[24,3072]{1,0:T(8,128)}, u32[]{:S(2)}) copy-start(f32[24,3072]{1,0:T(8,128)} %param.35) | copy-start | bytes 884740
  1033.9 370.0 %copy-start.52 = (f32[96,768]{1,0:T(8,128)S(1)}, f32[96,768]{1,0:T(8,128)}, u32[]{:S(2)}) copy-start(f32[96,768]{1,0:T(8,128)} %param.26) | copy-start | bytes 884740
  1033.9 370.0 %copy-start.71 = (f32[96,768]{1,0:T(8,128)S(1)}, f32[96,768]{1,0:T(8,128)}, u32[]{:S(2)}) copy-start(f32[96,768]{1,0:T(8,128)} %param.31) | copy-start | bytes 884740
  1033.9 370.0 %copy-start.72 = (f32[96,768]{1,0:T(8,128)S(1)}, f32[96,768]{1,0:T(8,128)}, u32[]{:S(2)}) copy-start(f32[96,768]{1,0:T(8,128)} %param.36) | copy-start | bytes 884740
  (106 other events, 3773.4 us)
Sparse Core Ops, SparseCore 0:
  11.5 62.8 all-gather.5
  77.9 125.2 all-gather.7
  206.7 66.0 all-gather.9
  276.1 61.9 all-gather.11
  756.4 168.4 reduce-scatter.4
  930.5 190.0 all-reduce.3
  1126.5 136.2 reduce-scatter.6
  1268.7 135.1 reduce-scatter.8
where the time goes:
time: 1420 us; the launch traced here: 1410 us
  waiting for transfers between devices  563 us (40%)
  matrix products  493 us (35%)
  other arithmetic  113 us (8%)
  blocking collectives  84.1 us (6%)
  starting transfers between devices  74.9 us (5%)
  local copies, waits for them, and re-layouts  69.7 us (5%)
  between operations  15.5 us (1%)
    ppermute x8, waiting for transfers between devices, shifted(): lax.ppermute(value, axis, [(source, source + steps) for source in range(i...  186 us
    reduce_scatter x1, waiting for transfers between devices, per_device(): lax.psum_scatter(grad_up, 'dev', scatter_dimension=0, tiled=True)  140 us
    reduce_scatter x1, waiting for transfers between devices, per_device(): lax.psum_scatter(grad_down, 'dev', scatter_dimension=0, tiled=True)  139 us
    dot_general x5, matrix products, attention_grads(): jnp.einsum('qhd,khd->hqk', grad_heads, value_heads, preferred_element_typ...  96.7 us
    unnamed x9, waiting for transfers between devices  85.1 us
    ppermute x8, starting transfers between devices, shifted(): lax.ppermute(value, axis, [(source, source + steps) for source in range(i...  74 us
    dot_general x5, matrix products, per_device(): jnp.einsum('hqk,khd->qhd', weights, kv_block[1].reshape(row_count, head_c...  73.4 us
    dot_general x5, matrix products, attention_grads(): jnp.einsum('hqk,qhd->khd', probs_low, grad_heads, preferred_element_type=...  70.5 us
  transfers between devices with their start and end apart: 16, of which 8 were waited for; matrix products, arithmetic and copies ran while one was open for 25% of the time, Pallas kernels for 0%

commit v1 on v0

v1 whole, which is shorter than its diff:
```python
import functools

import jax
import jax.numpy as jnp
from jax import lax
from jax.experimental import pallas as pl
from jax.experimental.pallas import tpu as pltpu
from jax.sharding import PartitionSpec as P

HD = 64
CLIP = 1500
STEP = 10
LANE = 128
FAR = 1 << 30
SQRT_HALF = 0.7071067811865476
INV_SQRT_TWO_PI = 0.3989422804014327


beta_one = 0.9
beta_two = 0.999
learn_rate = 0.02
weight_decay = 0.1
adam_eps = 1e-08
norm_eps = 1e-05
masked_score = -1e30
FORWARD_TILES = (256, 384)
QUERY_TILES = (256, 256)
KEY_TILES = (256, 256)
PROJECT_TILE = 768
MIDDLE_TILE = 256
MIDDLE_CHUNK = 512
LAST_TILE = 256
GROUP = 2
NT = (((1,), (1,)), ((), ()))
NN = (((1,), (0,)), ((), ()))


def shifted(value, axis, steps):
    count = lax.axis_size(axis)
    initial, last = (max(0, -steps), min(count, count - steps))
    return lax.ppermute(value, axis, [(source, source + steps) for source in range(initial, last)])


def dot(a, b, dims=NN):
    return lax.dot_general(a, b, dims, preferred_element_type=jnp.float32)


def stacked(pair, scale):
    lane = lax.broadcasted_iota(jnp.int32, pair.shape, 1)
    zero = jnp.zeros_like(pair)
    if scale is not None:
        pair = pair * jnp.asarray(scale, pair.dtype)
    return jnp.concatenate([jnp.where(lane < HD, pair, zero), jnp.where(lane >= HD, pair, zero)], axis=0)


def unstacked(both):
    rows = both.shape[0] // 2
    lane = lax.broadcasted_iota(jnp.int32, (rows, LANE), 1)
    return jnp.where(lane < HD, both[:rows], both[rows:])


def column(table, place):
    lane = lax.broadcasted_iota(jnp.int32, table.shape, 1)
    return jnp.sum(jnp.where(lane == place, table, 0.0), axis=1, keepdims=True)


def forward_kernel(tq, tk, pairs, bounds, lower, upper, q_ref, k_ref, v_ref, o_ref, lse_ref, qs, peak, acc):
    group = pl.program_id(0)
    tiles = q_ref.shape[0] // tq
    ones = jnp.ones((tk, LANE), jnp.bfloat16)

    @pl.when(group == 0)
    def _():
        lse_ref[...] = jnp.zeros_like(lse_ref)

    def one_tile(tile, none):
        rows = pl.ds(pl.multiple_of(tile * tq, tq), tq)
        for pair in range(pairs):
            qs[pair] = stacked(q_ref[rows, pair * LANE : (pair + 1) * LANE], HD ** -0.5)
        peak[...] = jnp.full_like(peak, masked_score)
        acc[...] = jnp.zeros_like(acc)
        low, high = lower[rows, :], upper[rows, :]

        def step(key_tile, none):
            first = pl.multiple_of(key_tile * tk, tk)
            places = first + lax.broadcasted_iota(jnp.int32, (tq, tk), 1)
            bias = jnp.where((places >= low) & (places < high), 0.0, masked_score)
            bias = jnp.concatenate([bias, bias], axis=0)
            for pair in range(pairs):
                lanes = slice(pair * LANE, (pair + 1) * LANE)
                scores = dot(qs[pair], k_ref[pl.ds(first, tk), lanes], NT) + bias
                old = peak[pair]
                new = jnp.maximum(old, jnp.max(scores, axis=1, keepdims=True))
                peak[pair] = new
                weights = jnp.exp(scores - new[:, :1]).astype(jnp.bfloat16)
                values = jnp.concatenate([v_ref[pl.ds(first, tk), lanes], ones], axis=1)
                scale = jnp.exp(old - new)
                acc[pair] = acc[pair] * jnp.concatenate([scale, scale], axis=1) + dot(weights, values)
            return none

        lax.fori_loop(bounds[2 * tile], bounds[2 * tile + 1], step, 0)
        lane = lax.broadcasted_iota(jnp.int32, (tq, LANE), 1)
        table = lse_ref[rows, :]
        for pair in range(pairs):
            both = acc[pair]
            total = both[:, LANE:]
            o_ref[rows, pair * LANE : (pair + 1) * LANE] = unstacked(both[:, :LANE] / total).astype(o_ref.dtype)
            logs = peak[pair] + jnp.log(total)
            head = (group * pairs + pair) * 2
            table = jnp.where(lane == head, logs[:tq], table)
            table = jnp.where(lane == head + 1, logs[tq:], table)
        lse_ref[rows, :] = table
        return none

    lax.fori_loop(0, tiles, one_tile, 0)


def attend(query, keys, values, lower, upper, bounds, tq, tk, pairs):
    rows, width = query.shape
    window = keys.shape[0]
    lanes = pairs * LANE
    return pl.pallas_call(
        functools.partial(forward_kernel, tq, tk, pairs),
        grid_spec=pltpu.PrefetchScalarGridSpec(
            num_scalar_prefetch=1, grid=(width // lanes,),
            in_specs=[
                pl.BlockSpec((rows, 1), lambda g, b: (0, 0)),
                pl.BlockSpec((rows, 1), lambda g, b: (0, 0)),
                pl.BlockSpec((rows, lanes), lambda g, b: (0, g)),
                pl.BlockSpec((window, lanes), lambda g, b: (0, g)),
                pl.BlockSpec((window, lanes), lambda g, b: (0, g)),
            ],
            out_specs=[pl.BlockSpec((rows, lanes), lambda g, b: (0, g)), pl.BlockSpec((rows, LANE), lambda g, b: (0, 0))],
            scratch_shapes=[
                pltpu.VMEM((pairs, 2 * tq, LANE), jnp.bfloat16),
                pltpu.VMEM((pairs, 2 * tq, LANE), jnp.float32),
                pltpu.VMEM((pairs, 2 * tq, 2 * LANE), jnp.float32),
            ],
        ),
        out_shape=[jax.ShapeDtypeStruct((rows, width), jnp.bfloat16), jax.ShapeDtypeStruct((rows, LANE), jnp.float32)],
        name="attend",
    )(bounds, lower, upper, query, keys, values)


def query_grad_kernel(tq, tk, pairs, bounds, lower, upper, q_ref, g_ref, k_ref, v_ref, lse_ref, delta_ref, dq_ref, qs, gs, logs, deltas, acc):
    group = pl.program_id(0)
    tiles = q_ref.shape[0] // tq

    def one_tile(tile, none):
        rows = pl.ds(pl.multiple_of(tile * tq, tq), tq)
        table, other = lse_ref[rows, :], delta_ref[rows, :]
        for pair in range(pairs):
            lanes = slice(pair * LANE, (pair + 1) * LANE)
            qs[pair] = stacked(q_ref[rows, lanes], HD ** -0.5)
            gs[pair] = stacked(g_ref[rows, lanes], None)
            head = (group * pairs + pair) * 2
            logs[pair] = jnp.broadcast_to(jnp.concatenate([column(table, head), column(table, head + 1)], axis=0), logs.shape[1:])
            deltas[pair] = jnp.broadcast_to(jnp.concatenate([column(other, head), column(other, head + 1)], axis=0), logs.shape[1:])
        acc[...] = jnp.zeros_like(acc)
        low, high = lower[rows, :], upper[rows, :]

        def step(key_tile, none):
            first = pl.multiple_of(key_tile * tk, tk)
            places = first + lax.broadcasted_iota(jnp.int32, (tq, tk), 1)
            bias = jnp.where((places >= low) & (places < high), 0.0, masked_score)
            bias = jnp.concatenate([bias, bias], axis=0)
            for pair in range(pairs):
                lanes = slice(pair * LANE, (pair + 1) * LANE)
                keys = k_ref[pl.ds(first, tk), lanes]
                scores = dot(qs[pair], keys, NT) + bias
                probs = jnp.exp(scores - logs[pair][:, :1])
                grad_probs = dot(gs[pair], v_ref[pl.ds(first, tk), lanes], NT)
                grad_scores = (probs * (grad_probs - deltas[pair][:, :1])).astype(jnp.bfloat16)
                acc[pair] += dot(grad_scores, keys)
            return none

        lax.fori_loop(bounds[2 * tile], bounds[2 * tile + 1], step, 0)
        for pair in range(pairs):
            dq_ref[rows, pair * LANE : (pair + 1) * LANE] = (unstacked(acc[pair]) * HD ** -0.5).astype(dq_ref.dtype)
        return none

    lax.fori_loop(0, tiles, one_tile, 0)


def query_grad(query, grad, keys, values, lse, delta, lower, upper, bounds, tq, tk, pairs):
    rows, width = query.shape
    window = keys.shape[0]
    lanes = pairs * LANE
    own = lambda: pl.BlockSpec((rows, lanes), lambda g, b: (0, g))
    far = lambda: pl.BlockSpec((window, lanes), lambda g, b: (0, g))
    fixed = lambda cols: pl.BlockSpec((rows, cols), lambda g, b: (0, 0))
    return pl.pallas_call(
        functools.partial(query_grad_kernel, tq, tk, pairs),
        grid_spec=pltpu.PrefetchScalarGridSpec(
            num_scalar_prefetch=1, grid=(width // lanes,),
            in_specs=[fixed(1), fixed(1), own(), own(), far(), far(), fixed(LANE), fixed(LANE)],
            out_specs=own(),
            scratch_shapes=[
                pltpu.VMEM((pairs, 2 * tq, LANE), jnp.bfloat16),
                pltpu.VMEM((pairs, 2 * tq, LANE), jnp.bfloat16),
                pltpu.VMEM((pairs, 2 * tq, LANE), jnp.float32),
                pltpu.VMEM((pairs, 2 * tq, LANE), jnp.float32),
                pltpu.VMEM((pairs, 2 * tq, LANE), jnp.float32),
            ],
        ),
        out_shape=jax.ShapeDtypeStruct((rows, width), jnp.bfloat16),
        name="query_grad",
    )(bounds, lower, upper, query, grad, keys, values, lse, delta)


def key_grad_kernel(tk, tq, pairs, base, bounds, lower, upper, k_ref, v_ref, q_ref, g_ref, lse_ref, delta_ref, dk_ref, dv_ref, ks, vs, acc):
    tiles = k_ref.shape[0] // tk

    def one_tile(tile, none):
        rows = pl.ds(pl.multiple_of(tile * tk, tk), tk)
        for pair in range(pairs):
            lanes = slice(pair * LANE, (pair + 1) * LANE)
            ks[pair] = stacked(k_ref[rows, lanes], HD ** -0.5)
            vs[pair] = stacked(v_ref[rows, lanes], None)
        acc[...] = jnp.zeros_like(acc)

        def step(query_tile, none):
            first = pl.multiple_of(query_tile * tq, tq)
            here = pl.ds(first, tq)
            places = base + tile * tk + lax.broadcasted_iota(jnp.int32, (tk, tq), 0)
            bias = jnp.where((places >= lower[:, here]) & (places < upper[:, here]), 0.0, masked_score)
            for pair in range(pairs):
                lanes = slice(pair * LANE, (pair + 1) * LANE)
                queries, grads = q_ref[here, lanes], g_ref[here, lanes]
                scores = dot(ks[pair], queries, NT)
                grad_probs = dot(vs[pair], grads, NT)
                probs, grad_scores = [], []
                for half in range(2):
                    part = slice(half * tk, (half + 1) * tk)
                    head = slice(2 * pair + half, 2 * pair + half + 1)
                    prob = jnp.exp(scores[part] + bias - lse_ref[0, head, here])
                    probs.append(prob.astype(jnp.bfloat16))
                    grad_scores.append((prob * (grad_probs[part] - delta_ref[0, head, here])).astype(jnp.bfloat16))
                acc[pair, :, :LANE] += dot(jnp.concatenate(grad_scores, axis=0), queries)
                acc[pair, :, LANE:] += dot(jnp.concatenate(probs, axis=0), grads)
            return none

        lax.fori_loop(bounds[2 * tile], bounds[2 * tile + 1], step, 0)
        for pair in range(pairs):
            lanes = slice(pair * LANE, (pair + 1) * LANE)
            dk_ref[rows, lanes] = (unstacked(acc[pair, :, :LANE]) * HD ** -0.5).astype(dk_ref.dtype)
            dv_ref[rows, lanes] = unstacked(acc[pair, :, LANE:]).astype(dv_ref.dtype)
        return none

    lax.fori_loop(0, tiles, one_tile, 0)


def key_grad(keys, values, query, grad, lse, delta, lower, upper, bounds, base, tk, tq, pairs):
    rows, width = keys.shape
    window = query.shape[0]
    lanes = pairs * LANE
    own = lambda: pl.BlockSpec((rows, lanes), lambda g, b: (0, g))
    far = lambda: pl.BlockSpec((window, lanes), lambda g, b: (0, g))
    line = lambda: pl.BlockSpec((1, window), lambda g, b: (0, 0))
    heads = lambda: pl.BlockSpec((1, 2 * pairs, window), lambda g, b: (g, 0, 0))
    return pl.pallas_call(
        functools.partial(key_grad_kernel, tk, tq, pairs, base),
        grid_spec=pltpu.PrefetchScalarGridSpec(
            num_scalar_prefetch=1, grid=(width // lanes,),
            in_specs=[line(), line(), own(), own(), far(), far(), heads(), heads()],
            out_specs=[own(), own()],
            scratch_shapes=[
                pltpu.VMEM((pairs, 2 * tk, LANE), jnp.bfloat16),
                pltpu.VMEM((pairs, 2 * tk, LANE), jnp.bfloat16),
                pltpu.VMEM((pairs, 2 * tk, 2 * LANE), jnp.float32),
            ],
        ),
        out_shape=[jax.ShapeDtypeStruct((rows, width), jnp.bfloat16)] * 2,
        name="key_grad",
    )(bounds, lower, upper, keys, values, query, grad, lse, delta)


def units(values):
    centre = values - jnp.mean(values, axis=-1, keepdims=True)
    inverse = lax.rsqrt(jnp.mean(centre * centre, axis=-1, keepdims=True) + norm_eps)
    return centre * inverse, inverse


def norm_pull(grad_output, unit, inverse, gain):
    grad_unit = grad_output * gain
    first = jnp.mean(grad_unit, axis=-1, keepdims=True)
    second = jnp.mean(grad_unit * unit, axis=-1, keepdims=True)
    return inverse * (grad_unit - first - unit * second)


def row_sum(values):
    return jnp.sum(values, axis=0, keepdims=True)


def gelu_pair(hidden):
    inner = 0.5 + 0.5 * lax.erf(hidden * SQRT_HALF)
    slope = inner + hidden * (jnp.exp(-0.5 * hidden * hidden) * INV_SQRT_TWO_PI)
    return hidden * inner, slope


def project_kernel(tile, active, tokens, vectors, weights, query, keys, values):
    place = pl.program_id(0)
    needed = (place >= active[0]) & (place < active[1])

    @pl.when(needed)
    def _():
        unit = units(tokens[...].astype(jnp.float32))[0]
        normed = (unit * vectors[0:1, :] + vectors[1:2, :]).astype(jnp.bfloat16)
        query[...] = (dot(normed, weights[0]) + vectors[2:3, :]).astype(query.dtype)
        keys[...] = dot(normed, weights[1]).astype(keys.dtype)
        values[...] = (dot(normed, weights[2]) + vectors[3:4, :]).astype(values.dtype)

    @pl.when(jnp.logical_not(needed))
    def _():
        for out in (query, keys, values):
            out[...] = jnp.zeros_like(out)


def project(tokens, vectors, weights, active, tile):
    rows, width = tokens.shape
    block = lambda: pl.BlockSpec((tile, width), lambda i, b: (i, 0))
    return pl.pallas_call(
        functools.partial(project_kernel, tile),
        grid_spec=pltpu.PrefetchScalarGridSpec(
            num_scalar_prefetch=1, grid=(rows // tile,),
            in_specs=[
                block(),
                pl.BlockSpec(vectors.shape, lambda i, b: (0, 0)),
                pl.BlockSpec(weights.shape, lambda i, b: (0, 0, 0)),
            ],
            out_specs=[block(), block(), block()],
        ),
        out_shape=[jax.ShapeDtypeStruct((rows, width), jnp.bfloat16)] * 3,
        name="project",
    )(active, tokens, vectors, weights)


def middle_kernel(tile, tokens, mixed, cotangent, vectors, up_bias, out_weight, up_weight, down_weight,
                  result, grad_middle, grad_mixed, delta, grad_out, grad_up, grad_down, grad_rows, grad_bias,
                  middle, normed, turned, total, back, actives, hiddens):
    place, count = pl.program_id(0), pl.num_programs(0)
    rows = tokens.shape[0]
    parts = [slice(i, i + tile) for i in range(0, rows, tile)]

    @pl.when(place == 0)
    def _():
        for part in parts:
            branch = dot(mixed[part, :], out_weight[...]) + vectors[4:5, :]
            wide = tokens[part, :].astype(jnp.float32) + branch
            middle[part, :] = wide
            unit = units(wide)[0]
            low = (unit * vectors[5:6, :] + vectors[6:7, :]).astype(jnp.bfloat16)
            normed[part, :] = low
            turned[:, part] = low.T
            total[part, :] = wide + vectors[7:8, :]
        back[...] = jnp.zeros_like(back)

    bias = jnp.zeros_like(grad_bias)
    for part in parts:
        hidden = dot(normed[part, :], up_weight[...]) + up_bias[...]
        wide, slope = gelu_pair(hidden)
        active = wide.astype(jnp.bfloat16)
        grad_active = dot(cotangent[part, :], down_weight[...], NT)
        grad_hidden = (grad_active * slope).astype(jnp.bfloat16)
        actives[part, :] = active
        hiddens[part, :] = grad_hidden
        bias += row_sum(grad_hidden.astype(jnp.float32))
        total[part, :] += dot(active, down_weight[...])
        back[part, :] += dot(grad_hidden, up_weight[...], NT)
    grad_bias[...] = bias
    grad_up[...] = dot(turned[...], hiddens[...]).astype(grad_up.dtype)
    grad_down[...] = dot(actives[...], cotangent[...], (((0,), (0,)), ((), ()))).astype(grad_down.dtype)

    @pl.when(place == count - 1)
    def _():
        sums = [jnp.zeros((1, tokens.shape[1]), jnp.float32) for _ in range(4)]
        for part in parts:
            result[part, :] = total[part, :].astype(result.dtype)
            unit, inverse = units(middle[part, :])
            incoming = back[part, :]
            wide = cotangent[part, :].astype(jnp.float32)
            grad = wide + norm_pull(incoming, unit, inverse, vectors[5:6, :])
            grad_middle[part, :] = grad
            branch = grad.astype(jnp.bfloat16)
            turned[:, part] = mixed[part, :].T
            hiddens_low = dot(branch, out_weight[...], NT).astype(jnp.bfloat16)
            grad_mixed[part, :] = hiddens_low
            product = hiddens_low.astype(jnp.float32) * mixed[part, :].astype(jnp.float32)
            delta[part, :] = head_sums(product)
            normed[part, :] = branch
            sums[0] += row_sum(branch.astype(jnp.float32))
            sums[1] += row_sum(incoming * unit)
            sums[2] += row_sum(incoming)
            sums[3] += row_sum(wide)
        grad_out[...] = dot(turned[...], normed[...]).astype(grad_out.dtype)
        grad_rows[...] = jnp.concatenate(sums + [jnp.zeros((4, tokens.shape[1]), jnp.float32)], axis=0)


def head_sums(product):
    rows, width = product.shape
    lane = lax.broadcasted_iota(jnp.int32, (rows, LANE), 1)
    table = jnp.zeros((rows, LANE), jnp.float32)
    for pair in range(width // LANE):
        piece = product[:, pair * LANE : (pair + 1) * LANE]
        first = jnp.sum(jnp.where(lane < HD, piece, 0.0), axis=1, keepdims=True)
        second = jnp.sum(jnp.where(lane >= HD, piece, 0.0), axis=1, keepdims=True)
        table = jnp.where(lane == 2 * pair, first, table)
        table = jnp.where(lane == 2 * pair + 1, second, table)
    return table


def middle_block(tokens, mixed, cotangent, vectors, up_bias, out_weight, up_weight, down_weight, tile, chunk):
    rows, width = tokens.shape
    hidden = up_weight.shape[1]
    whole = lambda shape: pl.BlockSpec(shape, lambda i: (0,) * len(shape))
    across = lambda r: pl.BlockSpec((r, chunk), lambda i: (0, i))
    down = lambda: pl.BlockSpec((chunk, width), lambda i: (i, 0))
    full = (rows, width)
    return pl.pallas_call(
        functools.partial(middle_kernel, tile),
        grid=(hidden // chunk,),
        in_specs=[whole(full), whole(full), whole(full), whole(vectors.shape), across(1), whole((width, width)), across(width), down()],
        out_specs=[whole(full), whole(full), whole(full), whole((rows, LANE)), whole((width, width)), across(width), down(), whole((8, width)), across(1)],
        out_shape=[
            jax.ShapeDtypeStruct(full, jnp.bfloat16),
            jax.ShapeDtypeStruct(full, jnp.float32),
            jax.ShapeDtypeStruct(full, jnp.bfloat16),
            jax.ShapeDtypeStruct((rows, LANE), jnp.float32),
            jax.ShapeDtypeStruct((width, width), jnp.bfloat16),
            jax.ShapeDtypeStruct((width, hidden), jnp.bfloat16),
            jax.ShapeDtypeStruct((hidden, width), jnp.bfloat16),
            jax.ShapeDtypeStruct((8, width), jnp.float32),
            jax.ShapeDtypeStruct((1, hidden), jnp.float32),
        ],
        scratch_shapes=[
            pltpu.VMEM(full, jnp.float32),
            pltpu.VMEM(full, jnp.bfloat16),
            pltpu.VMEM((width, rows), jnp.bfloat16),
            pltpu.VMEM(full, jnp.float32),
            pltpu.VMEM(full, jnp.float32),
            pltpu.VMEM((rows, chunk), jnp.bfloat16),
            pltpu.VMEM((rows, chunk), jnp.bfloat16),
        ],
        name="middle",
    )(tokens, mixed, cotangent, vectors, up_bias, out_weight, up_weight, down_weight)


def last_kernel(tile, tokens, grad_middle, grad_query, grad_keys, grad_values, vectors, weights,
                grad_tokens, grad_qkv, grad_rows, turned):
    rows, width = tokens.shape
    sums = [jnp.zeros((1, width), jnp.float32) for _ in range(4)]
    for first in range(0, rows, tile):
        part = slice(first, first + tile)
        unit, inverse = units(tokens[part, :].astype(jnp.float32))
        turned[:, part] = (unit * vectors[0:1, :] + vectors[1:2, :]).astype(jnp.bfloat16).T
        incoming = dot(grad_query[part, :], weights[0], NT)
        incoming += dot(grad_keys[part, :], weights[1], NT)
        incoming += dot(grad_values[part, :], weights[2], NT)
        grad_tokens[part, :] = grad_middle[part, :] + norm_pull(incoming, unit, inverse, vectors[0:1, :])
        sums[0] += row_sum(incoming * unit)
        sums[1] += row_sum(incoming)
        sums[2] += row_sum(grad_query[part, :].astype(jnp.float32))
        sums[3] += row_sum(grad_values[part, :].astype(jnp.float32))
    for place, grad in enumerate((grad_query, grad_keys, grad_values)):
        grad_qkv[place] = dot(turned[...], grad[...]).astype(grad_qkv.dtype)
    grad_rows[...] = jnp.concatenate(sums + [jnp.zeros((4, width), jnp.float32)], axis=0)


def last_block(tokens, grad_middle, grad_query, grad_keys, grad_values, vectors, weights, tile):
    rows, width = tokens.shape
    return pl.pallas_call(
        functools.partial(last_kernel, tile),
        out_shape=[
            jax.ShapeDtypeStruct((rows, width), jnp.float32),
            jax.ShapeDtypeStruct(weights.shape, jnp.bfloat16),
            jax.ShapeDtypeStruct((8, width), jnp.float32),
        ],
        scratch_shapes=[pltpu.VMEM((width, rows), jnp.bfloat16)],
        name="last",
    )(tokens, grad_middle, grad_query, grad_keys, grad_values, vectors, weights)


def adamw_step(master, gradient, first_moment, second_moment):
    first_new = beta_one * first_moment + (1.0 - beta_one) * gradient
    second_new = beta_two * second_moment + (1.0 - beta_two) * gradient * gradient
    fix_one = 1.0 - beta_one**STEP
    fix_two = 1.0 - beta_two**STEP
    update = -learn_rate * (
        first_new / fix_one / (jnp.sqrt(second_new / fix_two) + adam_eps) + weight_decay * master
    )
    return (update, first_new, second_new)


def per_device(
    tokens,
    cotangent,
    clip_start,
    clip_end,
    qkv_weight,
    out_weight,
    up_weight,
    down_weight,
    vectors,
    qkv_first,
    out_first,
    up_first,
    down_first,
    vector_first,
    qkv_second,
    out_second,
    up_second,
    down_second,
    vector_second,
):
    rows, width = tokens.shape
    device = lax.axis_index("dev")
    devices = lax.axis_size("dev")
    heads = width // HD
    reach = (rows + CLIP - 2) // rows
    base = reach * rows
    window_first = device * rows - base
    shards = (qkv_weight, out_weight, up_weight, down_weight, vectors)
    low = [shard.astype(jnp.bfloat16) for shard in shards]
    qkv_full = lax.all_gather(low[0], "dev", axis=1, tiled=True)
    out_full = lax.all_gather(low[1], "dev", axis=0, tiled=True)
    up_full = lax.all_gather(low[2], "dev", axis=0, tiled=True)
    down_full = lax.all_gather(low[3], "dev", axis=0, tiled=True)
    vector_full = lax.all_gather(low[4], "dev", axis=1, tiled=True).astype(jnp.float32)

    offsets = [offset for offset in range(-reach, reach + 1)]
    spans = jnp.stack([clip_start, clip_end])

    def windowed(value):
        return [value if offset == 0 else shifted(value, "dev", -offset) for offset in offsets]

    tokens_window = jnp.concatenate(windowed(tokens), axis=0)
    spans_window = jnp.concatenate(windowed(spans), axis=1)
    places = window_first + jnp.arange(spans_window.shape[1], dtype=jnp.int32)
    inside = (places >= 0) & (places < devices * rows)
    starts = jnp.where(inside, spans_window[0] - window_first, FAR)
    ends = jnp.where(inside, spans_window[1] - window_first, 0)
    own_start, own_end = clip_start - window_first, clip_end - window_first

    tq, tk = FORWARD_TILES
    forward_bounds = jnp.stack([own_start[::tq] // tk, (own_end[tq - 1 :: tq] + tk - 1) // tk], axis=1).reshape(-1)
    rq, rk = QUERY_TILES
    query_bounds = jnp.stack([own_start[::rq] // rk, (own_end[rq - 1 :: rq] + rk - 1) // rk], axis=1).reshape(-1)
    sk, sq = KEY_TILES
    last_keys = base + sk - 1 + jnp.arange(rows // sk, dtype=jnp.int32) * sk
    last_tiles = jnp.sum((starts[::sq][None, :] <= last_keys[:, None]).astype(jnp.int32), axis=1)
    first_tiles = own_start[::sk] // sq
    last_tiles = first_tiles + jnp.sum(((starts[::sq][None, :] <= last_keys[:, None]) & (jnp.arange(starts.shape[0] // sq)[None, :] >= first_tiles[:, None])).astype(jnp.int32), axis=1)
    key_bounds = jnp.stack([first_tiles, last_tiles], axis=1).reshape(-1)
    needed = jnp.stack([own_start[0] // PROJECT_TILE, (jnp.sum((inside & (starts < base + rows)).astype(jnp.int32)) + jnp.maximum(-window_first, 0) + PROJECT_TILE - 1) // PROJECT_TILE])

    query_window, key_window, value_window = project(tokens_window, vector_full, qkv_full, needed, PROJECT_TILE)
    own = lambda value: lax.slice_in_dim(value, base, base + rows, axis=0)
    query = own(query_window)
    lower, upper = own_start[:, None], own_end[:, None]
    mixed, lse = attend(query, key_window, value_window, lower, upper, forward_bounds, tq, tk, GROUP)
    up_bias = vector_full[8:].reshape(1, -1)
    (result, grad_middle, grad_mixed, delta, grad_out, grad_up, grad_down, middle_rows, bias_row) = middle_block(
        tokens, mixed, cotangent, vector_full, up_bias, out_full, up_full, down_full, MIDDLE_TILE, MIDDLE_CHUNK
    )
    table = jnp.concatenate([lse[:, :heads], delta[:, :heads]], axis=1).T
    grad_window = jnp.concatenate(windowed(grad_mixed), axis=0)
    table_window = jnp.concatenate(windowed(table), axis=1)
    groups = heads // (2 * GROUP)
    lse_window = table_window[:heads].reshape(groups, 2 * GROUP, -1)
    delta_window = table_window[heads:].reshape(groups, 2 * GROUP, -1)
    grad_query = query_grad(query, grad_mixed, key_window, value_window, lse, delta, lower, upper, query_bounds, rq, rk, GROUP)
    grad_keys, grad_values = key_grad(
        own(key_window), own(value_window), query_window, grad_window, lse_window, delta_window,
        starts[None, :], ends[None, :], key_bounds, base, sk, sq, GROUP,
    )
    grad_tokens, grad_qkv, last_rows = last_block(
        tokens, grad_middle, grad_query, grad_keys, grad_values, vector_full, qkv_full, LAST_TILE
    )
    grad_vectors = jnp.concatenate([last_rows[:4], middle_rows[:4], bias_row.reshape(-1, width)], axis=0)
    owned = (
        lax.psum_scatter(grad_qkv, "dev", scatter_dimension=1, tiled=True).astype(jnp.float32),
        lax.psum_scatter(grad_out, "dev", scatter_dimension=0, tiled=True).astype(jnp.float32),
        lax.psum_scatter(grad_up, "dev", scatter_dimension=0, tiled=True).astype(jnp.float32),
        lax.psum_scatter(grad_down, "dev", scatter_dimension=0, tiled=True).astype(jnp.float32),
        lax.psum_scatter(grad_vectors, "dev", scatter_dimension=1, tiled=True),
    )
    firsts = (qkv_first, out_first, up_first, down_first, vector_first)
    seconds = (qkv_second, out_second, up_second, down_second, vector_second)
    stepped = [adamw_step(*four) for four in zip(shards, owned, firsts, seconds)]
    return (result, grad_tokens) + tuple(stepped[place][kind] for kind in range(3) for place in range(5))


def solution(mesh):
    in_specs = (
        P("dev", None),
        P("dev", None),
        P("dev"),
        P("dev"),
        P(None, "dev", None),
        P("dev", None),
        P("dev", None),
        P("dev", None),
        P(None, "dev"),
        P(None, "dev", None),
        P("dev", None),
        P("dev", None),
        P("dev", None),
        P(None, "dev"),
        P(None, "dev", None),
        P("dev", None),
        P("dev", None),
        P("dev", None),
        P(None, "dev"),
    )
    out_specs = (
        P("dev", None),
        P("dev", None),
        P(None, "dev", None),
        P("dev", None),
        P("dev", None),
        P("dev", None),
        P(None, "dev"),
        P(None, "dev", None),
        P("dev", None),
        P("dev", None),
        P("dev", None),
        P(None, "dev"),
        P(None, "dev", None),
        P("dev", None),
        P("dev", None),
        P("dev", None),
        P(None, "dev"),
    )
    return jax.shard_map(
        per_device, mesh=mesh, in_specs=in_specs, out_specs=out_specs, check_vma=False
    )
```

time: 1420 us -> 872 us (0.61)
  matrix products: 493 us -> 0 us
  Pallas kernels: 0 us -> 205 us
  waiting for transfers between devices: 563 us -> 400 us
  other arithmetic: 113 us -> 21.3 us
  blocking collectives: 84.1 us -> 126 us
  starting transfers between devices: 74.9 us -> 47.4 us
  local copies, waits for them, and re-layouts: 69.7 us -> 51.1 us
    dot_general x42 -> x0, matrix products: 493 us -> none  [the longest x5 96.7 us: attention_grads(): jnp.einsum('qhd,khd->hqk', grad_heads, value_heads, preferred_element_typ...]
    pallas_call x0 -> x6, Pallas kernels: none -> 205 us  [the longest x1 50.7 us: query_grad(): pl.pallas_call(functools.partial(query_grad_kernel, tq, tk, pairs), grid_...]
    ppermute x8 -> x16, waiting for transfers between devices: 186 us -> 57.2 us  [shifted(): lax.ppermute(value, axis, [(source, source + steps) for source in range(i...]
    reduce_sum x11 -> x1, other arithmetic: 64.2 us -> 0.87 us  [per_device(): jnp.sum(((starts[::sq][None, :] <= last_keys[:, None]) & (jnp.arange(star...]
    all_gather x4, waiting for transfers between devices: 12.3 us -> 63.2 us  [the longest x1 63.2 us: per_device(): down_full = lax.all_gather(low[3], 'dev', axis=0, tiled=True)]
    reduce_scatter x1, waiting for transfers between devices: 140 us -> 110 us  [per_device(): lax.psum_scatter(grad_up, 'dev', scatter_dimension=0, tiled=True)]
    reduce_scatter x1, waiting for transfers between devices: 139 us -> 110 us  [per_device(): lax.psum_scatter(grad_down, 'dev', scatter_dimension=0, tiled=True)]
    ppermute x8 -> x16, starting transfers between devices: 74 us -> 47 us  [shifted(): lax.ppermute(value, axis, [(source, source + steps) for source in range(i...]
  transfers between devices with their start and end apart: 16 -> 24, of which waited for: 8 -> 8; matrix products, arithmetic and copies ran while one was open for 25% -> 8% of each run, Pallas kernels for 0% -> 19%
where the time goes in v1:
time: 872 us; the launch traced here: 868 us
  waiting for transfers between devices  400 us (46%)
  Pallas kernels  205 us (24%)
  blocking collectives  126 us (14%)
  local copies, waits for them, and re-layouts  51.1 us (6%)
  starting transfers between devices  47.4 us (5%)
  other arithmetic  21.3 us (2%)
  between operations  17.3 us (2%)
    reduce_scatter x1, waiting for transfers between devices, per_device(): lax.psum_scatter(grad_down, 'dev', scatter_dimension=0, tiled=True)  110 us
    reduce_scatter x1, waiting for transfers between devices, per_device(): lax.psum_scatter(grad_up, 'dev', scatter_dimension=0, tiled=True)  110 us
    all_gather x1, blocking collectives, per_device(): lax.all_gather(low[4], 'dev', axis=1, tiled=True).astype(jnp.float32)  68.1 us
    all_gather x1, waiting for transfers between devices, per_device(): down_full = lax.all_gather(low[3], 'dev', axis=0, tiled=True)  63.2 us
    unnamed x9, waiting for transfers between devices  59.7 us
    unnamed x1, blocking collectives  57.8 us
    ppermute x16, waiting for transfers between devices, shifted(): lax.ppermute(value, axis, [(source, source + steps) for source in range(i...  57.2 us
    pallas_call x1, Pallas kernels, query_grad(): pl.pallas_call(functools.partial(query_grad_kernel, tq, tk, pairs), grid_...  50.7 us
  transfers between devices with their start and end apart: 24, of which 8 were waited for; matrix products, arithmetic and copies ran while one was open for 8% of the time, Pallas kernels for 19%

profile of v1, /device:TPU:0, one launch (start us, length us, event | category | flops | bytes accessed | tf_op | source)
XLA Modules:
  0.0 867.6 jit_solution(2205338438861338960)
XLA Ops:
  15.4 5.5 collective-permute-start
  25.5 5.8 collective-permute-start.4
  32.9 68.1 %all-gather = bf16[32,24,12]{1,2,0:T(8,128)(2,1)S(1)} all-gather(bf16[1,24,12]{1,2,0:T(8,128)(2,1)S(1)} %convert_bitcast_fusion), channel_id=1, replica_groups=mesh['dev'=32] {'dev'}, dimensions={0}, use_global_device_ids=true | all-gather | bytes 19008 | tf_op jit(solution)/shard_map/all_gather | solution.py:528
  126.5 40.7 %collective-permute-done.7 = bf16[768,768]{1,0:T(8,128)(2,1)} collective-permute-done((bf16[768,768]{1,0:T(8,128)(2,1)}, bf16[768,768]{1,0:T(8,128)(2,1)}, u32[]{:S(2)}, u32[]{:S(2)}) %collective-permute-start.7) | collective-permute-done | bytes 1179680 | tf_op jit(solution)/shard_map/ppermute | solution.py:41
  169.6 15.3 %project.1 = (bf16[3840,768]{1,0:T(8,128)(2,1)}, bf16[3840,768]{1,0:T(8,128)(2,1)}, bf16[3840,768]{1,0:T(8,128)(2,1)}) custom-call(s32[2]{0:T(128)} %pad_add_fusion.4.active, bf16[3840,768]{1,0:T(8,128)(2,1)} %constant_dynamic-update-slice_fusion.5.tokens, f32[12,768]{1,0:T(8,128)} %bitcast.39, bf16[3,768,768]{2,1,0:T(8,128)(2,1)} %all-gather.6.cloned.1.call-done.weights), custom_call_target="tpu_custom_call" | custom-call | tf_op jit(solution)/shard_map/project/pallas_call | solution.py:322
  187.3 44.8 %attend.1 = (bf16[768,768]{1,0:T(8,128)(2,1)}, f32[768,128]{1,0:T(8,128)}) custom-call(s32[6]{0:T(128)} %reshape.91.bounds, s32[768,1]{1,0:T(8,128)} %broadcast_in_dim.23.lower, s32[768,1]{1,0:T(8,128)} %broadcast_in_dim.24.upper, bf16[768,768]{1,0:T(8,128)(2,1)} %slice.55.q_ref, bf16[3840,768]{1,0:T(8,128)(2,1)} %get-tuple-element.37.k_ref, ...), custom_call_target="tpu_custom_call" | custom-call | tf_op jit(solution)/shard_map/attend/pallas_call | solution.py:122
  233.2 63.2 %all-gather.12.cloned.1.call-done.down_weight = bf16[3072,768]{1,0:T(8,128)(2,1)} async-done(((bf16[96,768]{1,0:T(8,128)(2,1)}), bf16[3072,768]{1,0:T(8,128)(2,1)}) %all-gather.12.cloned.1.call-update) | async-done | bytes 4718608 | tf_op jit(solution)/shard_map/all_gather | solution.py:527
  296.4 35.9 %middle.1 = (bf16[768,768]{1,0:T(8,128)(2,1)}, f32[768,768]{1,0:T(8,128)}, bf16[768,768]{1,0:T(8,128)(2,1)}, f32[768,128]{1,0:T(8,128)}, bf16[768,768]{1,0:T(8,1...) custom-call(bf16[768,768]{1,0:T(8,128)(2,1)} %tokens.3, ...), custom_call_target="tpu_custom_call" | custom-call | tf_op jit(solution)/shard_map/middle/pallas_call | solution.py:419
  334.1 3.9 collective-permute-start.12
  341.8 2.4 slice.60.v_ref
  344.3 3.8 collective-permute-start.8
  352.4 50.7 %query_grad.1.grad_query = bf16[768,768]{1,0:T(8,128)(2,1)} custom-call(s32[6]{0:T(128)} %reshape.93.bounds, s32[768,1]{1,0:T(8,128)} %broadcast_in_dim.23.lower, s32[768,1]{1,0:T(8,128)} %broadcast_in_dim.24.upper, bf16[768,768]{1,0:T(8,128)(2,1)} %slice.55.q_ref, bf16[768,768]{1,0:T(8,128)(2,1)} %get-tuple-element.42.g_ref, ...), custom_call_target="tpu_custom_call" | custom-call | tf_op jit(solution)/shard_map/query_grad/pallas_call | solution.py:192
  403.2 11.7 %collective-permute-start.13 = (f32[24,768]{1,0:T(8,128)}, f32[24,768]{1,0:T(8,128)S(1)}, u32[]{:S(2)}, u32[]{:S(2)}) collective-permute-start(f32[24,768]{1,0:T(8,128)} %maximum_bitcast_fusion), channel_id=1, source_target_pairs={{0,1},{1,2},{2,3},{3,4},{4,5},{5,6},{6,7},{7,8},{8,9},{9,10},{10,1... | collective-permute-start | bytes 221192 | tf_op jit(solution)/shard_map/ppermute | solution.py:41
  418.2 9.7 %collective-permute-done.14 = f32[24,768]{1,0:T(8,128)S(1)} collective-permute-done((f32[24,768]{1,0:T(8,128)}, f32[24,768]{1,0:T(8,128)S(1)}, u32[]{:S(2)}, u32[]{:S(2)}) %collective-permute-start.14) | collective-permute-done | bytes 73760 | tf_op jit(solution)/shard_map/ppermute | solution.py:41
  429.4 6.5 collective-permute-done.15
  443.6 2.4 constant_dynamic-update-slice_fusion.12
  448.2 45.8 %key_grad.1 = (bf16[768,768]{1,0:T(8,128)(2,1)}, bf16[768,768]{1,0:T(8,128)(2,1)}) custom-call(s32[6]{0:T(128)} %reshape.94.bounds, s32[1,3840]{1,0:T(1,128)} %get-tuple-element.73.lower, s32[1,3840]{1,0:T(1,128)} %get-tuple-element.72.upper, bf16[768,768]{1,0:T(8,128)(2,1)} %slice.59.k_ref, bf16[768,768]{1,0:T(8,128)(2,1)} %slice.60.v_ref, ...), custom_call_target="tpu_custom_call" | custom-call | tf_op jit(solution)/shard_map/key_grad/pallas_call | solution.py:261
  493.9 12.2 %last.1 = (f32[768,768]{1,0:T(8,128)}, bf16[3,768,768]{2,1,0:T(8,128)(2,1)}, f32[8,768]{1,0:T(8,128)}) custom-call(bf16[768,768]{1,0:T(8,128)(2,1)} %tokens.3, f32[768,768]{1,0:T(8,128)} %get-tuple-element.41.grad_middle, bf16[768,768]{1,0:T(8,128)(2,1)} %query_grad.1.grad_query, bf16[768,768]{1,0:T(8,128)(2,1)} %get-tuple-element.45.grad_keys, ...), custom_call_target="tpu_custom_call" | custom-call | tf_op jit(solution)/shard_map/last/pallas_call | solution.py:471
  506.1 5.1 copy.83
  511.1 2.5 copy.88
  516.6 57.8 %all-reduce = f32[12,768]{1,0:T(8,128)S(1)} all-reduce(f32[12,768]{1,0:T(8,128)S(1)} %pad_maximum_fusion), channel_id=6, replica_groups=mesh['dev'=32] {'dev'}, use_global_device_ids=true, to_apply=%region_6.7.clone | all-reduce | flops 9216 | bytes 73728
  576.6 58.3 %reduce-scatter.14.cloned.1.call-done = bf16[24,2304]{1,0:T(8,128)(2,1)} async-done(((bf16[768,2304]{1,0:T(8,128)(2,1)}), bf16[24,2304]{1,0:T(8,128)(2,1)}) %reduce-scatter.14.cloned.1.call-update) | async-done | bytes 110608
  636.9 109.8 %reduce-scatter.10.cloned.1.call-done = bf16[24,3072]{1,0:T(8,128)(2,1)} async-done(((bf16[768,3072]{1,0:T(8,128)(2,1)}), bf16[24,3072]{1,0:T(8,128)(2,1)}) %reduce-scatter.10.cloned.1.call-update) | async-done | bytes 147472 | tf_op jit(solution)/shard_map/reduce_scatter | solution.py:583
  748.6 110.1 %reduce-scatter.12.cloned.1.call-done = bf16[96,768]{1,0:T(8,128)(2,1)} async-done(((bf16[3072,768]{1,0:T(8,128)(2,1)}), bf16[96,768]{1,0:T(8,128)(2,1)}) %reduce-scatter.12.cloned.1.call-update) | async-done | bytes 147472 | tf_op jit(solution)/shard_map/reduce_scatter | solution.py:584
  (163 shorter events, 78.3 us)
Async XLA Ops:
  7.2 162.4 %all-gather.6.cloned.1.call-start = ((), (), s32[]{:S(2)}) async-start(), calls=%async_computation.4 | async-start | bytes 3649536 | tf_op jit(solution)/shard_map/all_gather | solution.py:524
  9.0 224.3 %all-gather.8.cloned.1.call-start = ((), (), s32[]{:S(2)}) async-start(), calls=%async_computation.5 | async-start | bytes 1216512 | tf_op jit(solution)/shard_map/all_gather | solution.py:525
  10.5 222.7 %all-gather.10.cloned.1.call-start = ((), (), s32[]{:S(2)}) async-start(), calls=%async_computation.6 | async-start | bytes 4866048 | tf_op jit(solution)/shard_map/all_gather | solution.py:526
  12.2 284.2 %all-gather.12.cloned.1.call-start = ((), (), s32[]{:S(2)}) async-start(), calls=%async_computation.7 | async-start | bytes 4866048 | tf_op jit(solution)/shard_map/all_gather | solution.py:527
  14.0 561.2 %reduce-scatter.8.cloned.1.call-start = ((), (), s32[]{:S(2)}) async-start(), calls=%async_computation.8 | async-start | bytes 1216512 | tf_op jit(solution)/shard_map/reduce_scatter | solution.py:582
  15.4 93.1 %collective-permute-start = (s32[2,768]{1,0:T(2,128)S(1)}, s32[2,768]{1,0:T(2,128)}, u32[]{:S(2)}, u32[]{:S(2)}) collective-permute-start(s32[2,768]{1,0:T(2,128)S(1)} %pad_add_fusion), channel_id=1, source_target_pairs={{0,2},{1,3},{2,4},{3,5},{4,6},{5,7},{6,8},{7,9},{8,10},{9,11},{10,... | collective-permute-start | bytes 18440 | tf_op jit(solution)/shard_map/ppermute | solution.py:41
  20.9 90.5 %collective-permute-start.1 = (s32[2,768]{1,0:T(2,128)S(1)}, s32[2,768]{1,0:T(2,128)}, u32[]{:S(2)}, u32[]{:S(2)}) collective-permute-start(s32[2,768]{1,0:T(2,128)S(1)} %pad_add_fusion), channel_id=1, source_target_pairs={{0,1},{1,2},{2,3},{3,4},{4,5},{5,6},{6,7},{7,8},{8,9},{9,10},{10,1... | collective-permute-start | bytes 18440 | tf_op jit(solution)/shard_map/ppermute | solution.py:41
  22.9 90.5 %collective-permute-start.2 = (s32[2,768]{1,0:T(2,128)S(1)}, s32[2,768]{1,0:T(2,128)}, u32[]{:S(2)}, u32[]{:S(2)}) collective-permute-start(s32[2,768]{1,0:T(2,128)S(1)} %pad_add_fusion), channel_id=1, source_target_pairs={{1,0},{2,1},{3,2},{4,3},{5,4},{6,5},{7,6},{8,7},{9,8},{10,9},{11,1... | collective-permute-start | bytes 18440 | tf_op jit(solution)/shard_map/ppermute | solution.py:41
  24.2 91.2 %collective-permute-start.3 = (s32[2,768]{1,0:T(2,128)S(1)}, s32[2,768]{1,0:T(2,128)}, u32[]{:S(2)}, u32[]{:S(2)}) collective-permute-start(s32[2,768]{1,0:T(2,128)S(1)} %pad_add_fusion), channel_id=1, source_target_pairs={{2,0},{3,1},{4,2},{5,3},{6,4},{7,5},{8,6},{9,7},{10,8},{11,9},{12,... | collective-permute-start | bytes 18440 | tf_op jit(solution)/shard_map/ppermute | solution.py:41
  25.5 95.3 %collective-permute-start.4 = (bf16[768,768]{1,0:T(8,128)(2,1)}, bf16[768,768]{1,0:T(8,128)(2,1)S(1)}, u32[]{:S(2)}, u32[]{:S(2)}) collective-permute-start(bf16[768,768]{1,0:T(8,128)(2,1)} %tokens.3), channel_id=1, source_target_pairs={{0,2},{1,3},{2,4},{3,5},{4,6},{5,7},{6,8},{7,9},{8,10},{9,11},{10,... | collective-permute-start | bytes 3538952 | tf_op jit(solution)/shard_map/ppermute | solution.py:41
  108.5 13.3 %collective-permute-start.5 = (bf16[768,768]{1,0:T(8,128)(2,1)}, bf16[768,768]{1,0:T(8,128)(2,1)S(1)}, u32[]{:S(2)}, u32[]{:S(2)}) collective-permute-start(bf16[768,768]{1,0:T(8,128)(2,1)} %tokens.3), channel_id=1, source_target_pairs={{0,1},{1,2},{2,3},{3,4},{4,5},{5,6},{6,7},{7,8},{8,9},{9,10},{10,1... | collective-permute-start | bytes 3538952 | tf_op jit(solution)/shard_map/ppermute | solution.py:41
  111.4 12.7 %collective-permute-start.6 = (bf16[768,768]{1,0:T(8,128)(2,1)}, bf16[768,768]{1,0:T(8,128)(2,1)}, u32[]{:S(2)}, u32[]{:S(2)}) collective-permute-start(bf16[768,768]{1,0:T(8,128)(2,1)} %tokens.3), channel_id=1, source_target_pairs={{1,0},{2,1},{3,2},{4,3},{5,4},{6,5},{7,6},{8,7},{9,8},{10,9},{11,1... | collective-permute-start | bytes 3538952 | tf_op jit(solution)/shard_map/ppermute | solution.py:41
  113.4 53.8 %collective-permute-start.7 = (bf16[768,768]{1,0:T(8,128)(2,1)}, bf16[768,768]{1,0:T(8,128)(2,1)}, u32[]{:S(2)}, u32[]{:S(2)}) collective-permute-start(bf16[768,768]{1,0:T(8,128)(2,1)} %tokens.3), channel_id=1, source_target_pairs={{2,0},{3,1},{4,2},{5,3},{6,4},{7,5},{8,6},{9,7},{10,8},{11,9},{12,... | collective-permute-start | bytes 3538952 | tf_op jit(solution)/shard_map/ppermute | solution.py:41
  334.1 69.1 %collective-permute-start.12 = (f32[24,768]{1,0:T(8,128)}, f32[24,768]{1,0:T(8,128)}, u32[]{:S(2)}, u32[]{:S(2)}) collective-permute-start(f32[24,768]{1,0:T(8,128)} %maximum_bitcast_fusion), channel_id=1, source_target_pairs={{0,2},{1,3},{2,4},{3,5},{4,6},{5,7},{6,8},{7,9},{8,10},{9,11},{10,... | collective-permute-start | bytes 221192 | tf_op jit(solution)/shard_map/ppermute | solution.py:41
  344.3 95.8 %collective-permute-start.8 = (bf16[768,768]{1,0:T(8,128)(2,1)}, bf16[768,768]{1,0:T(8,128)(2,1)}, u32[]{:S(2)}, u32[]{:S(2)}) collective-permute-start(bf16[768,768]{1,0:T(8,128)(2,1)} %get-tuple-element.42.g_ref), channel_id=1, source_target_pairs={{0,2},{1,3},{2,4},{3,5},{4,6},{5,7},{6,8},{7,9},{8,10},{9,11},{10,... | collective-permute-start | bytes 3538952 | tf_op jit(solution)/shard_map/ppermute | solution.py:41
  348.1 94.3 %collective-permute-start.9 = (bf16[768,768]{1,0:T(8,128)(2,1)}, bf16[768,768]{1,0:T(8,128)(2,1)S(1)}, u32[]{:S(2)}, u32[]{:S(2)}) collective-permute-start(bf16[768,768]{1,0:T(8,128)(2,1)} %get-tuple-element.42.g_ref), channel_id=1, source_target_pairs={{0,1},{1,2},{2,3},{3,4},{4,5},{5,6},{6,7},{7,8},{8,9},{9,10},{10,1... | collective-permute-start | bytes 3538952 | tf_op jit(solution)/shard_map/ppermute | solution.py:41
  349.8 96.2 %collective-permute-start.10 = (bf16[768,768]{1,0:T(8,128)(2,1)}, bf16[768,768]{1,0:T(8,128)(2,1)S(1)}, u32[]{:S(2)}, u32[]{:S(2)}) collective-permute-start(bf16[768,768]{1,0:T(8,128)(2,1)} %get-tuple-element.42.g_ref), channel_id=1, source_target_pairs={{1,0},{2,1},{3,2},{4,3},{5,4},{6,5},{7,6},{8,7},{9,8},{10,9},{11,1... | collective-permute-start | bytes 3538952 | tf_op jit(solution)/shard_map/ppermute | solution.py:41
  351.1 96.0 %collective-permute-start.11 = (bf16[768,768]{1,0:T(8,128)(2,1)}, bf16[768,768]{1,0:T(8,128)(2,1)S(1)}, u32[]{:S(2)}, u32[]{:S(2)}) collective-permute-start(bf16[768,768]{1,0:T(8,128)(2,1)} %get-tuple-element.42.g_ref), channel_id=1, source_target_pairs={{2,0},{3,1},{4,2},{5,3},{6,4},{7,5},{8,6},{9,7},{10,8},{11,9},{12,... | collective-permute-start | bytes 3538952 | tf_op jit(solution)/shard_map/ppermute | solution.py:41
  403.1 231.8 %reduce-scatter.14.cloned.1.call-start = ((), (), s32[]{:S(2)}) async-start(), calls=%async_computation.11 | async-start | bytes 3649536
  403.2 12.8 %collective-permute-start.13 = (f32[24,768]{1,0:T(8,128)}, f32[24,768]{1,0:T(8,128)S(1)}, u32[]{:S(2)}, u32[]{:S(2)}) collective-permute-start(f32[24,768]{1,0:T(8,128)} %maximum_bitcast_fusion), channel_id=1, source_target_pairs={{0,1},{1,2},{2,3},{3,4},{4,5},{5,6},{6,7},{7,8},{8,9},{9,10},{10,1... | collective-permute-start | bytes 221192 | tf_op jit(solution)/shard_map/ppermute | solution.py:41
  416.0 11.9 %collective-permute-start.14 = (f32[24,768]{1,0:T(8,128)}, f32[24,768]{1,0:T(8,128)S(1)}, u32[]{:S(2)}, u32[]{:S(2)}) collective-permute-start(f32[24,768]{1,0:T(8,128)} %maximum_bitcast_fusion), channel_id=1, source_target_pairs={{1,0},{2,1},{3,2},{4,3},{5,4},{6,5},{7,6},{8,7},{9,8},{10,9},{11,1... | collective-permute-start | bytes 221192 | tf_op jit(solution)/shard_map/ppermute | solution.py:41
  427.9 8.0 collective-permute-start.15
  513.7 233.0 %reduce-scatter.10.cloned.1.call-start = ((), (), s32[]{:S(2)}) async-start(), calls=%async_computation.9 | async-start | bytes 4866048 | tf_op jit(solution)/shard_map/reduce_scatter | solution.py:583
  514.5 344.2 %reduce-scatter.12.cloned.1.call-start = ((), (), s32[]{:S(2)}) async-start(), calls=%async_computation.10 | async-start | bytes 4866048 | tf_op jit(solution)/shard_map/reduce_scatter | solution.py:584
  (22 other events, 2675.1 us)
Sparse Core Ops, SparseCore 0:
  11.5 69.1 all-gather.5
  84.2 54.0 all-gather.7
  141.8 89.2 all-gather.9
  234.5 61.9 all-gather.11
  403.3 110.2 reduce-scatter.7
  518.8 116.0 reduce-scatter.13
  640.4 106.1 reduce-scatter.9
  752.1 106.5 reduce-scatter.11

commit v2 on v1

--- a/solution.py
+++ b/solution.py
@@ -31,6 +31,12 @@
 MIDDLE_CHUNK = 512
 LAST_TILE = 256
 GROUP = 2
+CHUNK_BYTES = 40000
+PER_STEP = 4
+HALO_START = 0
+HALO_PASS = 3
+GATHER_ORDERS = ((0, 1, 2), (0, 2, 1))
+SCATTER_ORDERS = ((2, 1, 0), (1, 2, 0))
 NT = (((1,), (1,)), ((), ()))
 NN = (((1,), (0,)), ((), ()))
 
@@ -480,6 +486,382 @@
     )(tokens, grad_middle, grad_query, grad_keys, grad_values, vectors, weights)
 
 
+def chip_axes(devices):
+    chips = devices // 2
+    return {16: (4, 2, 2), 64: (4, 4, 4)}.get(chips, (chips, 1, 1))
+
+
+class Place:
+    def __init__(self, dims):
+        self.dims = dims
+        self.me = lax.axis_index("dev")
+        self.core = lax.rem(self.me, 2)
+        chip = self.me // 2
+        self.at = (chip // (dims[1] * dims[2]), lax.rem(chip // dims[2], dims[1]), lax.rem(chip, dims[2]))
+        self.partner = self.me + 1 - 2 * self.core
+
+    def peer(self, axis, step):
+        there = lax.rem(self.at[axis] + step, self.dims[axis])
+        at = [there if a == axis else self.at[a] for a in range(3)]
+        return ((at[0] * self.dims[1] + at[1]) * self.dims[2] + at[2]) * 2 + self.core, there
+
+    def peers(self):
+        return [self.partner] + [self.peer(axis, step)[0] for axis in range(3) for step in range(1, self.dims[axis])]
+
+
+def remote(source, target, send, recv, device):
+    return pltpu.make_async_remote_copy(
+        src_ref=source, dst_ref=target, send_sem=send, recv_sem=recv,
+        device_id=(device,), device_id_type=pl.DeviceIdType.MESH,
+    )
+
+
+def greet(peers, around=None, devices=0):
+    barrier = pltpu.get_barrier_semaphore()
+    count = len(peers)
+    for peer in peers:
+        pl.semaphore_signal(barrier, inc=1, device_id=(peer,), device_id_type=pl.DeviceIdType.MESH)
+    if around is not None:
+        for other in (around - 2, around + 2):
+            there = (other >= 0) & (other < devices)
+            count = count + there.astype(jnp.int32)
+
+            @pl.when(there)
+            def _():
+                pl.semaphore_signal(barrier, inc=1, device_id=(other,), device_id_type=pl.DeviceIdType.MESH)
+
+    pl.semaphore_wait(barrier, count)
+
+
+class Halo:
+    def __init__(self, place, devices, own, window, send, recv, local):
+        self.place, self.devices, self.own, self.window = place, devices, own, window
+        self.send, self.recv, self.local = send, recv, local
+        me, core = place.me, place.core
+        self.above, self.below = me + 2 < devices, me >= 2
+        self.up = remote(own, window.at[0], send.at[0], recv.at[0], me + 2)
+        self.down = remote(own, window.at[4], send.at[1], recv.at[1], me - 2)
+        side = jnp.where(core == 0, 1, 3)
+        self.across = remote(own, window.at[side], send.at[2], recv.at[2], place.partner)
+        self.kept = jnp.where(core == 0, 4, 0)
+        self.relay = remote(window.at[self.kept], window.at[4 - side], send.at[3], recv.at[3], place.partner)
+        self.keep = pltpu.make_async_copy(own, window.at[2], local)
+
+    def start(self):
+        pl.when(self.above)(self.up.start)
+        pl.when(self.below)(self.down.start)
+        self.across.start()
+        self.keep.start()
+
+    def pass_on(self):
+        pl.when(self.below)(self.up.wait_recv)
+        pl.when(self.above)(self.down.wait_recv)
+        even = self.place.core == 0
+        self.relays = jnp.where(even, self.above, self.below)
+        pl.when(self.relays)(self.relay.start)
+
+    def finish(self):
+        even = self.place.core == 0
+        comes = jnp.where(even, self.below, self.above)
+        self.across.wait_recv()
+        pl.when(comes)(self.relay.wait_recv)
+        self.keep.wait()
+        pl.when(self.above)(self.up.wait_send)
+        pl.when(self.below)(self.down.wait_send)
+        self.across.wait_send()
+        pl.when(self.relays)(self.relay.wait_send)
+
+
+def gather_kernel(dims, devices, chunks, orders, arrays, halos, *refs):
+    shards, owns = refs[:arrays], refs[arrays : arrays + halos]
+    fulls = refs[arrays + halos : 2 * arrays + halos]
+    windows = refs[2 * arrays + halos : 2 * (arrays + halos)]
+    send, recv, local, halo_send, halo_recv, halo_local = refs[2 * (arrays + halos) :]
+    place = Place(dims)
+    greet(place.peers(), place.me, devices)
+    parts = [
+        Halo(place, devices, owns[i], windows[i], halo_send.at[i], halo_recv.at[i], halo_local.at[i])
+        for i in range(halos)
+    ]
+    count = len(chunks)
+    started = {}
+
+    def stage(number, level):
+        array, lead, lanes = chunks[number]
+        shard, full = shards[array], fulls[array]
+        front = () if lead is None else (lead,)
+        source = shard.at[front + (slice(None), lanes)] if front else shard.at[:, lanes]
+        order = orders[number]
+        done = order[: min(level, 3)]
+        index = tuple(slice(None) if axis in done else place.at[axis] for axis in range(3))
+        view = lambda index, core: full.at[front + index + (core, slice(None), lanes)]
+        if level == 0:
+            mine = pltpu.make_async_copy(source, view(index, place.core), local.at[number])
+            mine.start()
+            started[number] = [mine]
+        else:
+            for copy in started[number, level - 1]:
+                copy.wait_recv()
+            if level == 1:
+                started[number][0].wait()
+            source = view(index, place.core)
+        copies = []
+        if level == 3:
+            copies.append(remote(source, source, send.at[number, 0], recv.at[number, 0], place.partner))
+        else:
+            base = 1 + sum(dims[axis] - 1 for axis in order[:level])
+            for step in range(1, dims[order[level]]):
+                slot = base + step - 1
+                device = place.peer(order[level], step)[0]
+                target = view(index, place.core)
+                copies.append(remote(source, target, send.at[number, slot], recv.at[number, slot], device))
+        for copy in copies:
+            copy.start()
+        started[number, level] = copies
+
+    steps = -(-count // PER_STEP)
+    for time in range(steps + 3):
+        for level in (3, 2, 1, 0):
+            for number in range((time - level) * PER_STEP, (time - level + 1) * PER_STEP):
+                if 0 <= number < count:
+                    stage(number, level)
+        if time == HALO_START:
+            for part in parts:
+                part.start()
+        if time == min(HALO_PASS, steps + 2):
+            for part in parts:
+                part.pass_on()
+    for number in range(count):
+        for copy in started[number, 3]:
+            copy.wait_recv()
+        for level in range(4):
+            for copy in started[number, level]:
+                copy.wait_send()
+    for part in parts:
+        part.finish()
+
+
+def gather(shards, owns, devices):
+    dims = chip_axes(devices)
+    chunks = []
+    for array, shard in enumerate(shards):
+        lanes = shard.shape[-1]
+        if shard.ndim == 3:
+            chunks += [(array, lead, slice(0, lanes)) for lead in range(shard.shape[0])]
+        else:
+            wide = min(lanes, max(CHUNK_BYTES // (2 * shard.shape[0]) // LANE * LANE, LANE))
+            wide = max(w for w in range(LANE, wide + 1, LANE) if lanes % w == 0)
+            chunks += [(array, None, slice(first, first + wide)) for first in range(0, lanes, wide)]
+    orders = [GATHER_ORDERS[number % len(GATHER_ORDERS)] for number in range(len(chunks))]
+    slots = 1 + sum(size - 1 for size in dims)
+    anywhere = pl.BlockSpec(memory_space=pl.ANY)
+    inside = pl.BlockSpec(memory_space=pltpu.VMEM)
+    outs = [
+        jax.ShapeDtypeStruct(shard.shape[:-2] + dims + (2,) + shard.shape[-2:], shard.dtype) for shard in shards
+    ] + [jax.ShapeDtypeStruct((5,) + own.shape, own.dtype) for own in owns]
+    done = pl.pallas_call(
+        functools.partial(gather_kernel, dims, devices, chunks, orders, len(shards), len(owns)),
+        in_specs=[inside] * (len(shards) + len(owns)),
+        out_specs=[anywhere] * len(outs),
+        out_shape=outs,
+        scratch_shapes=[
+            pltpu.SemaphoreType.DMA((len(chunks), slots)),
+            pltpu.SemaphoreType.DMA((len(chunks), slots)),
+            pltpu.SemaphoreType.DMA((len(chunks),)),
+            pltpu.SemaphoreType.DMA((max(len(owns), 1), 4)),
+            pltpu.SemaphoreType.DMA((max(len(owns), 1), 4)),
+            pltpu.SemaphoreType.DMA((max(len(owns), 1),)),
+        ],
+        compiler_params=pltpu.CompilerParams(collective_id=0, has_side_effects=True),
+        name="gather",
+    )(*shards, *owns)
+    return done[: len(shards)], done[len(shards) :]
+
+
+def halo_kernel(dims, devices, halos, *refs):
+    owns, windows = refs[:halos], refs[halos : 2 * halos]
+    send, recv, local = refs[2 * halos :]
+    place = Place(dims)
+    greet([place.partner], place.me, devices)
+    parts = [Halo(place, devices, owns[i], windows[i], send.at[i], recv.at[i], local.at[i]) for i in range(halos)]
+    for part in parts:
+        part.start()
+    for part in parts:
+        part.pass_on()
+    for part in parts:
+        part.finish()
+
+
+def halo(owns, devices):
+    outs = [jax.ShapeDtypeStruct((5,) + own.shape, own.dtype) for own in owns]
+    return pl.pallas_call(
+        functools.partial(halo_kernel, chip_axes(devices), devices, len(owns)),
+        in_specs=[pl.BlockSpec(memory_space=pltpu.VMEM)] * len(owns),
+        out_specs=[pl.BlockSpec(memory_space=pl.ANY)] * len(owns),
+        out_shape=outs,
+        scratch_shapes=[
+            pltpu.SemaphoreType.DMA((len(owns), 4)),
+            pltpu.SemaphoreType.DMA((len(owns), 4)),
+            pltpu.SemaphoreType.DMA((len(owns),)),
+        ],
+        compiler_params=pltpu.CompilerParams(collective_id=1, has_side_effects=True),
+        name="halo",
+    )(*owns)
+
+
+def scatter_kernel(dims, chunks, arrays, orders, *refs):
+    grads, outs = refs[:arrays], refs[arrays : 2 * arrays]
+    rest = refs[2 * arrays :]
+    count = len(chunks)
+    buffers = [rest[5 * i : 5 * i + 5] for i in range(count)]
+    send, recv, local = rest[5 * count :]
+    place = Place(dims)
+    greet(place.peers())
+    started = {}
+
+    def source(number, core):
+        array, lead, lanes = chunks[number]
+        front = () if lead is None else (lead,)
+        return grads[array].at[front + (slice(None), slice(None), slice(None), core, slice(None), lanes)]
+
+    def spread(shape, one):
+        total = 1
+        for size in shape:
+            total *= size
+
+        def body(flat, none):
+            index = []
+            for size in reversed(shape):
+                index.insert(0, lax.rem(flat, size))
+                flat = flat // size
+            one(tuple(index))
+            return none
+
+        lax.fori_loop(0, total, body, 0)
+
+    def stage(number, level):
+        own, first, second, third, fourth = buffers[number]
+        order = orders[number]
+        held = (own, second, third, fourth)
+        copies = []
+        if level == 0:
+            mine = pltpu.make_async_copy(source(number, place.core), own, local.at[number])
+            mine.start()
+            started[number] = mine
+            copies.append(remote(source(number, 1 - place.core), first, send.at[number, 0], recv.at[number, 0], place.partner))
+        else:
+            for copy in started[number, level - 1]:
+                copy.wait_recv()
+            remaining = [axis for axis in range(3) if axis not in order[: level - 1]]
+            if level == 1:
+                started[number].wait()
+
+                def add(index):
+                    total = own[index].astype(jnp.float32) + first[index].astype(jnp.float32)
+                    own[index] = total.astype(own.dtype)
+
+                spread(dims, add)
+            else:
+                combine(number, level)
+            axis = order[level - 1]
+            base = 1 + sum(dims[a] - 1 for a in order[: level - 1])
+            for step in range(1, dims[axis]):
+                device, there = place.peer(axis, step)
+                where = tuple(there if a == axis else slice(None) for a in remaining)
+                slot = base + step - 1
+                piece = (own if level == 1 else held[level - 1].at[0]).at[where]
+                copies.append(remote(piece, held[level].at[step - 1], send.at[number, slot], recv.at[number, slot], device))
+        for copy in copies:
+            copy.start()
+        started[number, level] = copies
+
+    def combine(number, level):
+        own, first, second, third, fourth = buffers[number]
+        order = orders[number]
+        held = (own, second, third, fourth)
+        axis = order[level - 2]
+        before = [a for a in range(3) if a not in order[: level - 2]]
+        after = [a for a in before if a != axis]
+        slots = dims[axis] - 1
+        old = own if level == 2 else held[level - 2].at[0]
+        new = held[level - 1]
+        array, lead, lanes = chunks[number]
+
+        def add(index):
+            where = list(index)
+            where.insert(before.index(axis), place.at[axis])
+            total = old[tuple(where)].astype(jnp.float32)
+            for slot in range(slots):
+                total += new[(slot,) + index].astype(jnp.float32)
+            if level == 4:
+                if lead is None:
+                    outs[array][:, lanes] = total
+                else:
+                    outs[array][lead, :, lanes] = total
+            else:
+                new[(0,) + index] = total.astype(new.dtype)
+
+        if after:
+            spread([dims[a] for a in after], add)
+        else:
+            add(())
+
+    for time in range(-(-count // PER_STEP) + 4):
+        for level in (4, 3, 2, 1, 0):
+            for number in range((time - level) * PER_STEP, (time - level + 1) * PER_STEP):
+                if not 0 <= number < count:
+                    continue
+                if level == 4:
+                    for copy in started[number, 3]:
+                        copy.wait_recv()
+                    combine(number, 4)
+                else:
+                    stage(number, level)
+    for number in range(count):
+        for level in range(4):
+            for copy in started[number, level]:
+                copy.wait_send()
+
+
+def scatter(grads, devices):
+    dims = chip_axes(devices)
+    chunks = []
+    for array, grad in enumerate(grads):
+        rows, lanes = grad.shape[-2:]
+        if grad.ndim == 7:
+            chunks += [(array, lead, slice(0, lanes)) for lead in range(grad.shape[0])]
+        else:
+            wide = min(lanes, max(CHUNK_BYTES // (2 * rows) // LANE * LANE, LANE))
+            wide = max(w for w in range(LANE, wide + 1, LANE) if lanes % w == 0)
+            chunks += [(array, None, slice(first, first + wide)) for first in range(0, lanes, wide)]
+    orders = [SCATTER_ORDERS[number % len(SCATTER_ORDERS)] for number in range(len(chunks))]
+    scratch = []
+    for (array, lead, lanes), order in zip(chunks, orders):
+        grad = grads[array]
+        piece = (grad.shape[-2], lanes.stop - lanes.start)
+        left = [dims[a] for a in range(3)]
+        scratch += [pltpu.VMEM(dims + piece, grad.dtype)] * 2
+        remaining = [0, 1, 2]
+        for axis in order:
+            remaining.remove(axis)
+            scratch.append(pltpu.VMEM((max(dims[axis] - 1, 1),) + tuple(dims[a] for a in remaining) + piece, grad.dtype))
+    slots = 1 + sum(size - 1 for size in dims)
+    outs = [jax.ShapeDtypeStruct(grad.shape[:-6] + grad.shape[-2:], jnp.float32) for grad in grads]
+    return pl.pallas_call(
+        functools.partial(scatter_kernel, dims, chunks, len(grads), orders),
+        in_specs=[pl.BlockSpec(memory_space=pl.ANY)] * len(grads),
+        out_specs=[pl.BlockSpec(memory_space=pltpu.VMEM)] * len(grads),
+        out_shape=outs,
+        scratch_shapes=scratch + [
+            pltpu.SemaphoreType.DMA((len(chunks), slots)),
+            pltpu.SemaphoreType.DMA((len(chunks), slots)),
+            pltpu.SemaphoreType.DMA((len(chunks),)),
+        ],
+        compiler_params=pltpu.CompilerParams(collective_id=2, has_side_effects=True),
+        name="scatter",
+    )(*grads)
+
+
 def adamw_step(master, gradient, first_moment, second_moment):
     first_new = beta_one * first_moment + (1.0 - beta_one) * gradient
     second_new = beta_two * second_moment + (1.0 - beta_two) * gradient * gradient
@@ -521,20 +903,17 @@
     window_first = device * rows - base
     shards = (qkv_weight, out_weight, up_weight, down_weight, vectors)
     low = [shard.astype(jnp.bfloat16) for shard in shards]
-    qkv_full = lax.all_gather(low[0], "dev", axis=1, tiled=True)
-    out_full = lax.all_gather(low[1], "dev", axis=0, tiled=True)
-    up_full = lax.all_gather(low[2], "dev", axis=0, tiled=True)
-    down_full = lax.all_gather(low[3], "dev", axis=0, tiled=True)
-    vector_full = lax.all_gather(low[4], "dev", axis=1, tiled=True).astype(jnp.float32)
-
-    offsets = [offset for offset in range(-reach, reach + 1)]
-    spans = jnp.stack([clip_start, clip_end])
-
-    def windowed(value):
-        return [value if offset == 0 else shifted(value, "dev", -offset) for offset in offsets]
-
-    tokens_window = jnp.concatenate(windowed(tokens), axis=0)
-    spans_window = jnp.concatenate(windowed(spans), axis=1)
+    vector_part = jnp.pad(low[4].T, ((0, 0), (0, LANE - vectors.shape[0])))
+    spans = jnp.pad(jnp.stack([clip_start, clip_end]), ((0, 6), (0, 0)))
+    fulls, (tokens_window, spans_window) = gather(low[:1] + [vector_part] + low[1:4], [tokens, spans], devices)
+    dims = chip_axes(devices)
+    qkv_full = fulls[0].reshape(-1, width, width)
+    vector_full = fulls[1].reshape(width, LANE)[:, : vectors.shape[0]].T.astype(jnp.float32)
+    out_full = fulls[2].reshape(width, width)
+    up_full = fulls[3].reshape(width, -1)
+    down_full = fulls[4].reshape(-1, width)
+    tokens_window = tokens_window.reshape(-1, width)
+    spans_window = spans_window.transpose(1, 0, 2).reshape(8, -1)
     places = window_first + jnp.arange(spans_window.shape[1], dtype=jnp.int32)
     inside = (places >= 0) & (places < devices * rows)
     starts = jnp.where(inside, spans_window[0] - window_first, FAR)
@@ -563,8 +942,9 @@
         tokens, mixed, cotangent, vector_full, up_bias, out_full, up_full, down_full, MIDDLE_TILE, MIDDLE_CHUNK
     )
     table = jnp.concatenate([lse[:, :heads], delta[:, :heads]], axis=1).T
-    grad_window = jnp.concatenate(windowed(grad_mixed), axis=0)
-    table_window = jnp.concatenate(windowed(table), axis=1)
+    grad_window, table_window = halo([grad_mixed, table], devices)
+    grad_window = grad_window.reshape(-1, width)
+    table_window = table_window.transpose(1, 0, 2).reshape(2 * heads, -1)
     groups = heads // (2 * GROUP)
     lse_window = table_window[:heads].reshape(groups, 2 * GROUP, -1)
     delta_window = table_window[heads:].reshape(groups, 2 * GROUP, -1)
@@ -577,13 +957,11 @@
         tokens, grad_middle, grad_query, grad_keys, grad_values, vector_full, qkv_full, LAST_TILE
     )
     grad_vectors = jnp.concatenate([last_rows[:4], middle_rows[:4], bias_row.reshape(-1, width)], axis=0)
-    owned = (
-        lax.psum_scatter(grad_qkv, "dev", scatter_dimension=1, tiled=True).astype(jnp.float32),
-        lax.psum_scatter(grad_out, "dev", scatter_dimension=0, tiled=True).astype(jnp.float32),
-        lax.psum_scatter(grad_up, "dev", scatter_dimension=0, tiled=True).astype(jnp.float32),
-        lax.psum_scatter(grad_down, "dev", scatter_dimension=0, tiled=True).astype(jnp.float32),
-        lax.psum_scatter(grad_vectors, "dev", scatter_dimension=1, tiled=True),
-    )
+    spread = lambda grad, lead=(): grad.reshape(lead + dims + (2, grad.shape[len(lead)] // devices, grad.shape[-1]))
+    vector_rows = grad_vectors.reshape(vectors.shape[0], devices, -1).transpose(1, 0, 2).reshape(devices, -1)
+    vector_rows = jnp.pad(vector_rows, ((0, 0), (0, 8 * LANE - vector_rows.shape[1]))).reshape(dims + (2, 8, LANE))
+    owned = scatter([spread(grad_up), spread(grad_down), spread(grad_out), spread(grad_qkv, (3,)), vector_rows], devices)
+    owned = (owned[3], owned[2], owned[0], owned[1], owned[4].reshape(-1)[: vectors.size].reshape(vectors.shape))
     firsts = (qkv_first, out_first, up_first, down_first, vector_first)
     seconds = (qkv_second, out_second, up_second, down_second, vector_second)
     stepped = [adamw_step(*four) for four in zip(shards, owned, firsts, seconds)]

time: 872 us -> 560 us (0.64)
  waiting for transfers between devices: 400 us -> 0 us
  Pallas kernels: 205 us -> 511 us
  blocking collectives: 126 us -> 0 us
  starting transfers between devices: 47.4 us -> 0 us
  local copies, waits for them, and re-layouts: 51.1 us -> 23.7 us
  between operations: 17.3 us -> 3.74 us
    pallas_call x0 -> x3, Pallas kernels: none -> 306 us  [the longest x1 124 us: gather(): pl.pallas_call(functools.partial(gather_kernel, dims, devices, chunks, or...]
    reduce_scatter x3 -> x0, waiting for transfers between devices: 220 us -> none  [the longest x1 110 us: per_device(): lax.psum_scatter(grad_down, 'dev', scatter_dimension=0, tiled=True)]
    all_gather x1 -> x0, blocking collectives: 68.1 us -> none  [per_device(): lax.all_gather(low[4], 'dev', axis=1, tiled=True).astype(jnp.float32)]
    all_gather x4 -> x0, waiting for transfers between devices: 63.2 us -> none  [the longest x1 63.2 us: per_device(): down_full = lax.all_gather(low[3], 'dev', axis=0, tiled=True)]
    unnamed x9 -> x0, waiting for transfers between devices: 59.7 us -> none
    unnamed x1 -> x0, blocking collectives: 57.8 us -> none
    ppermute x16 -> x0, waiting for transfers between devices: 57.2 us -> none  [shifted(): lax.ppermute(value, axis, [(source, source + steps) for source in range(i...]
    ppermute x16 -> x0, starting transfers between devices: 47 us -> none  [shifted(): lax.ppermute(value, axis, [(source, source + steps) for source in range(i...]
  transfers between devices with their start and end apart: 24 -> 0, of which waited for: 8 -> 0; matrix products, arithmetic and copies ran while one was open for 8% -> 0% of each run, Pallas kernels for 19% -> 0%
where the time goes in v2:
time: 560 us; the launch traced here: 557 us
  Pallas kernels  511 us (91%)
  local copies, waits for them, and re-layouts  23.7 us (4%)
  other arithmetic  18.7 us (3%)
    pallas_call x1, Pallas kernels, gather(): pl.pallas_call(functools.partial(gather_kernel, dims, devices, chunks, or...  124 us
    pallas_call x1, Pallas kernels, scatter(): pl.pallas_call(functools.partial(scatter_kernel, dims, chunks, len(grads)...  97.8 us
    pallas_call x1, Pallas kernels, halo(): pl.pallas_call(functools.partial(halo_kernel, chip_axes(devices), devices...  83.8 us
    pallas_call x1, Pallas kernels, query_grad(): pl.pallas_call(functools.partial(query_grad_kernel, tq, tk, pairs), grid_...  50.8 us
    pallas_call x1, Pallas kernels, key_grad(): pl.pallas_call(functools.partial(key_grad_kernel, tk, tq, pairs, base), g...  46 us
    pallas_call x1, Pallas kernels, attend(): pl.pallas_call(functools.partial(forward_kernel, tq, tk, pairs), grid_spe...  44.8 us
    pallas_call x1, Pallas kernels, middle_block(): pl.pallas_call(functools.partial(middle_kernel, tile), grid=(hidden // ch...  35.9 us
    pallas_call x1, Pallas kernels, project(): pl.pallas_call(functools.partial(project_kernel, tile), grid_spec=pltpu.P...  15.4 us

profile of v2, /device:TPU:0, one launch (start us, length us, event | category | flops | bytes accessed | tf_op | source)
XLA Modules:
  0.0 557.0 jit_solution(450871798563011258)
XLA Ops:
  0.7 1.6 convert_element_type.34.refs_3_
  2.3 1.6 convert_element_type.35.refs_4_
  4.0 1.6 convert_element_type.31.refs_0_
  5.6 1.5 convert_element_type.33.refs_2_
  10.5 124.3 %gather.1 = (bf16[3,4,2,2,2,24,768]{6,5,4,3,2,1,0:T(8,128)(2,1)}, bf16[4,2,2,2,24,128]{5,4,3,2,1,0:T(8,128)(2,1)}, bf16[4,2,2,2,24,768]{5,4,3,2,1,0:T(8,128)(2,1...) custom-call(bf16[3,24,768]{2,1,0:T(8,128)(2,1)} %convert_element_typ, ...), custom_call_target="tpu_custom_call" | custom-call | tf_op jit(solution)/shard_map/gather/pallas_call | solution.py:662
  134.8 1.7 fusion.14
  140.3 1.0 copy.91
  142.0 15.4 %project.1 = (bf16[3840,768]{1,0:T(8,128)(2,1)}, bf16[3840,768]{1,0:T(8,128)(2,1)}, bf16[3840,768]{1,0:T(8,128)(2,1)}) custom-call(s32[2]{0:T(128)} %pad_add_fusion.4.active, bf16[3840,768]{1,0:T(8,128)(2,1)} %bitcast.48, f32[12,768]{1,0:T(8,128)} %convert_bitcast_fusion.vectors, bf16[3,768,768]{2,1,0:T(8,128)(2,1)} %bitcast.46), custom_call_target="tpu_custom_call" | custom-call | tf_op jit(solution)/shard_map/project/pallas_call | solution.py:328
  157.4 2.4 slice.66.q_ref
  161.6 0.9 broadcast_in_dim.27.upper
  162.5 44.8 %attend.1 = (bf16[768,768]{1,0:T(8,128)(2,1)}, f32[768,128]{1,0:T(8,128)}) custom-call(s32[6]{0:T(128)} %reshape.204.bounds, s32[768,1]{1,0:T(8,128)} %broadcast_in_dim.26.lower, s32[768,1]{1,0:T(8,128)} %broadcast_in_dim.27.upper, bf16[768,768]{1,0:T(8,128)(2,1)} %slice.66.q_ref, bf16[3840,768]{1,0:T(8,128)(2,1)} %get-tuple-element.55.k_ref, ...), custom_call_target="tpu_custom_call" | custom-call | tf_op jit(solution)/shard_map/attend/pallas_call | solution.py:128
  208.6 35.9 %middle.1 = (bf16[768,768]{1,0:T(8,128)(2,1)}, f32[768,768]{1,0:T(8,128)}, bf16[768,768]{1,0:T(8,128)(2,1)}, f32[768,128]{1,0:T(8,128)}, bf16[768,768]{1,0:T(8,1...) custom-call(bf16[768,768]{1,0:T(8,128)(2,1)} %tokens.3, ...), custom_call_target="tpu_custom_call" | custom-call | tf_op jit(solution)/shard_map/middle/pallas_call | solution.py:425
  244.5 1.2 copy.86
  246.5 83.8 %halo.1 = (bf16[5,768,768]{2,1,0:T(8,128)(2,1)}, f32[5,24,768]{2,1,0:T(8,128)}) custom-call(bf16[768,768]{1,0:T(8,128)(2,1)} %get-tuple-element.63.g_ref.refs_0_, f32[24,768]{1,0:T(8,128)} %maximum_bitcast_fusion.1.refs_1_), custom_call_target="tpu_custom_call" | custom-call | tf_op jit(solution)/shard_map/halo/pallas_call | solution.py:697
  330.3 1.1 fusion.20
  333.2 2.4 slice.70.k_ref
  335.6 2.4 slice.71.v_ref
  339.7 46.0 %key_grad.1 = (bf16[768,768]{1,0:T(8,128)(2,1)}, bf16[768,768]{1,0:T(8,128)(2,1)}) custom-call(s32[6]{0:T(128)} %reshape.213.bounds, s32[1,3840]{1,0:T(1,128)} %get-tuple-element.110.lower, s32[1,3840]{1,0:T(1,128)} %get-tuple-element.111.upper, bf16[768,768]{1,0:T(8,128)(2,1)} %slice.70.k_ref, bf16[768,768]{1,0:T(8,128)(2,1)} %slice.71.v_ref, ...), custom_call_target="tpu_custom_call" | custom-call | tf_op jit(solution)/shard_map/key_grad/pallas_call | solution.py:267
  386.3 50.8 %query_grad.1.grad_query = bf16[768,768]{1,0:T(8,128)(2,1)} custom-call(s32[6]{0:T(128)} %reshape.212.bounds, s32[768,1]{1,0:T(8,128)} %broadcast_in_dim.26.lower, s32[768,1]{1,0:T(8,128)} %broadcast_in_dim.27.upper, bf16[768,768]{1,0:T(8,128)(2,1)} %slice.66.q_ref, bf16[768,768]{1,0:T(8,128)(2,1)} %get-tuple-element.63.g_ref.refs_0_, ...), custom_call_target="tpu_custom_call" | custom-call | tf_op jit(solution)/shard_map/query_grad/pallas_call | solution.py:198
  437.1 12.1 %last.1 = (f32[768,768]{1,0:T(8,128)}, bf16[3,768,768]{2,1,0:T(8,128)(2,1)}, f32[8,768]{1,0:T(8,128)}) custom-call(bf16[768,768]{1,0:T(8,128)(2,1)} %tokens.3, f32[768,768]{1,0:T(8,128)} %get-tuple-element.62.grad_middle, bf16[768,768]{1,0:T(8,128)(2,1)} %query_grad.1.grad_query, bf16[768,768]{1,0:T(8,128)(2,1)} %get-tuple-element.68.grad_keys, ...), custom_call_target="tpu_custom_call" | custom-call | tf_op jit(solution)/shard_map/last/pallas_call | solution.py:477
  452.4 97.8 %scatter.1 = (f32[24,3072]{1,0:T(8,128)}, f32[96,768]{1,0:T(8,128)}, f32[24,768]{1,0:T(8,128)}, f32[3,24,768]{2,1,0:T(8,128)}, f32[8,128]{1,0:T(8,128)}) custom-call(bf16[4,2,2,2,24,3072]{5,4,3,2,1,0:T(8,128)(2,1)} %bitcast.50, bf16[4,2,2,2,96,768]{5,4,3,2,1,0:T(8,128)(2,1)} %bitcast.51, bf16[4,2,2,2,24,768]{5,4,3,2,1,0:T(8,128)(2,1)} %bitcast.55, ...), custom_call_target="tpu_custom_call" | custom-call | tf_op jit(solution)/shard_map/scatter/pallas_call | solution.py:850
  550.3 2.2 add_multiply_fusion
  552.5 2.0 add_multiply_fusion.1
  554.6 0.9 add_multiply_fusion.2
  (103 shorter events, 17.9 us)
Async XLA Ops:
  0.7 136.5 %copy-start.17 = (s32[768]{0:T(1024)S(1)}, s32[768]{0:T(1024)}, u32[]{:S(2)}) copy-start(s32[768]{0:T(1024)} %param.21) | copy-start | bytes 9220
  0.7 136.5 %copy-start.16 = (s32[768]{0:T(1024)S(1)}, s32[768]{0:T(1024)}, u32[]{:S(2)}) copy-start(s32[768]{0:T(1024)} %param.22) | copy-start | bytes 9220
  208.6 37.1 %copy-start = (f32[768,128]{1,0:T(8,128)S(1)}, f32[768,128]{1,0:T(8,128)}, u32[]{:S(2)}) copy-start(f32[768,128]{1,0:T(8,128)} %get-tuple-element.64.lse_ref) | copy-start | bytes 1179652
  437.1 13.5 %copy-start.18 = (f32[1,3072]{1,0:T(1,128)S(1)}, f32[1,3072]{1,0:T(1,128)}, u32[]{:S(2)}) copy-start(f32[1,3072]{1,0:T(1,128)} %get-tuple-element.77) | copy-start | bytes 36868
  437.1 14.2 %copy-start.21 = (f32[8,768]{1,0:T(8,128)S(1)}, f32[8,768]{1,0:T(8,128)}, u32[]{:S(2)}) copy-start(f32[8,768]{1,0:T(8,128)} %get-tuple-element.76) | copy-start | bytes 73732
  452.4 97.9 %copy-start.1 = (f32[96,768]{1,0:T(8,128)S(1)}, f32[96,768]{1,0:T(8,128)}, u32[]{:S(2)}) copy-start(f32[96,768]{1,0:T(8,128)} %param.26) | copy-start | bytes 884740
  452.4 97.9 %copy-start.5 = (f32[96,768]{1,0:T(8,128)S(1)}, f32[96,768]{1,0:T(8,128)}, u32[]{:S(2)}) copy-start(f32[96,768]{1,0:T(8,128)} %param.31) | copy-start | bytes 884740
  452.4 97.9 %copy-start.6 = (f32[96,768]{1,0:T(8,128)S(1)}, f32[96,768]{1,0:T(8,128)}, u32[]{:S(2)}) copy-start(f32[96,768]{1,0:T(8,128)} %param.36) | copy-start | bytes 884740
  452.4 100.1 %copy-start.2 = (f32[24,3072]{1,0:T(8,128)S(1)}, f32[24,3072]{1,0:T(8,128)}, u32[]{:S(2)}) copy-start(f32[24,3072]{1,0:T(8,128)} %param.25) | copy-start | bytes 884740
  452.4 100.1 %copy-start.7 = (f32[24,3072]{1,0:T(8,128)S(1)}, f32[24,3072]{1,0:T(8,128)}, u32[]{:S(2)}) copy-start(f32[24,3072]{1,0:T(8,128)} %param.30) | copy-start | bytes 884740
  452.4 100.1 %copy-start.8 = (f32[24,3072]{1,0:T(8,128)S(1)}, f32[24,3072]{1,0:T(8,128)}, u32[]{:S(2)}) copy-start(f32[24,3072]{1,0:T(8,128)} %param.35) | copy-start | bytes 884740
  550.2 4.3 copy-start.3
  550.2 4.3 copy-start.9
  550.2 4.3 copy-start.10
  550.3 4.3 copy-start.11
  550.3 5.2 copy-start.4
  550.3 5.2 copy-start.12
  550.3 5.2 copy-start.13
  550.3 5.2 copy-start.14
  552.5 3.7 copy-start.22
  552.5 3.8 copy-start.15
  552.5 3.8 copy-start.19
  552.5 3.8 copy-start.20

commit v3 on v2

--- a/solution.py
+++ b/solution.py
@@ -37,6 +37,10 @@
 HALO_PASS = 3
 GATHER_ORDERS = ((0, 1, 2), (0, 2, 1))
 SCATTER_ORDERS = ((2, 1, 0), (1, 2, 0))
+EXCHANGE_ORDERS = ((1, 2, 0), (1, 2, 0), (2, 1, 0))
+SCATTER_PASS = 3
+GATHER_LEVELS = (0, 1, 2, 3)
+SCATTER_LEVELS = (0, 1, 2, 3, 4)
 NT = (((1,), (1,)), ((), ()))
 NN = (((1,), (0,)), ((), ()))
 
@@ -98,7 +102,7 @@
                 old = peak[pair]
                 new = jnp.maximum(old, jnp.max(scores, axis=1, keepdims=True))
                 peak[pair] = new
-                weights = jnp.exp(scores - new[:, :1]).astype(jnp.bfloat16)
+                weights = jnp.exp(scores - jnp.concatenate([new] * (tk // LANE), axis=1)).astype(jnp.bfloat16)
                 values = jnp.concatenate([v_ref[pl.ds(first, tk), lanes], ones], axis=1)
                 scale = jnp.exp(old - new)
                 acc[pair] = acc[pair] * jnp.concatenate([scale, scale], axis=1) + dot(weights, values)
@@ -122,8 +126,8 @@
 
 
 def attend(query, keys, values, lower, upper, bounds, tq, tk, pairs):
-    rows, width = query.shape
-    window = keys.shape[0]
+    rows, (window, width) = lower.shape[0], keys.shape
+    middle = window // rows // 2
     lanes = pairs * LANE
     return pl.pallas_call(
         functools.partial(forward_kernel, tq, tk, pairs),
@@ -132,7 +136,7 @@
             in_specs=[
                 pl.BlockSpec((rows, 1), lambda g, b: (0, 0)),
                 pl.BlockSpec((rows, 1), lambda g, b: (0, 0)),
-                pl.BlockSpec((rows, lanes), lambda g, b: (0, g)),
+                pl.BlockSpec((rows, lanes), lambda g, b: (middle, g)),
                 pl.BlockSpec((window, lanes), lambda g, b: (0, g)),
                 pl.BlockSpec((window, lanes), lambda g, b: (0, g)),
             ],
@@ -174,9 +178,9 @@
                 lanes = slice(pair * LANE, (pair + 1) * LANE)
                 keys = k_ref[pl.ds(first, tk), lanes]
                 scores = dot(qs[pair], keys, NT) + bias
-                probs = jnp.exp(scores - logs[pair][:, :1])
+                probs = jnp.exp(scores - jnp.concatenate([logs[pair]] * (tk // LANE), axis=1))
                 grad_probs = dot(gs[pair], v_ref[pl.ds(first, tk), lanes], NT)
-                grad_scores = (probs * (grad_probs - deltas[pair][:, :1])).astype(jnp.bfloat16)
+                grad_scores = (probs * (grad_probs - jnp.concatenate([deltas[pair]] * (tk // LANE), axis=1))).astype(jnp.bfloat16)
                 acc[pair] += dot(grad_scores, keys)
             return none
 
@@ -189,17 +193,17 @@
 
 
 def query_grad(query, grad, keys, values, lse, delta, lower, upper, bounds, tq, tk, pairs):
-    rows, width = query.shape
-    window = keys.shape[0]
+    (rows, width), window = grad.shape, keys.shape[0]
+    middle = window // rows // 2
     lanes = pairs * LANE
-    own = lambda: pl.BlockSpec((rows, lanes), lambda g, b: (0, g))
+    own = lambda at=0: pl.BlockSpec((rows, lanes), lambda g, b: (at, g))
     far = lambda: pl.BlockSpec((window, lanes), lambda g, b: (0, g))
     fixed = lambda cols: pl.BlockSpec((rows, cols), lambda g, b: (0, 0))
     return pl.pallas_call(
         functools.partial(query_grad_kernel, tq, tk, pairs),
         grid_spec=pltpu.PrefetchScalarGridSpec(
             num_scalar_prefetch=1, grid=(width // lanes,),
-            in_specs=[fixed(1), fixed(1), own(), own(), far(), far(), fixed(LANE), fixed(LANE)],
+            in_specs=[fixed(1), fixed(1), own(middle), own(), far(), far(), fixed(LANE), fixed(LANE)],
             out_specs=own(),
             scratch_shapes=[
                 pltpu.VMEM((pairs, 2 * tq, LANE), jnp.bfloat16),
@@ -256,11 +260,11 @@
     lax.fori_loop(0, tiles, one_tile, 0)
 
 
-def key_grad(keys, values, query, grad, lse, delta, lower, upper, bounds, base, tk, tq, pairs):
-    rows, width = keys.shape
-    window = query.shape[0]
+def key_grad(keys, values, query, grad, lse, delta, lower, upper, bounds, base, rows, tk, tq, pairs):
+    window, width = query.shape
+    middle = base // rows
     lanes = pairs * LANE
-    own = lambda: pl.BlockSpec((rows, lanes), lambda g, b: (0, g))
+    own = lambda at=0: pl.BlockSpec((rows, lanes), lambda g, b: (at, g))
     far = lambda: pl.BlockSpec((window, lanes), lambda g, b: (0, g))
     line = lambda: pl.BlockSpec((1, window), lambda g, b: (0, 0))
     heads = lambda: pl.BlockSpec((1, 2 * pairs, window), lambda g, b: (g, 0, 0))
@@ -268,7 +272,7 @@
         functools.partial(key_grad_kernel, tk, tq, pairs, base),
         grid_spec=pltpu.PrefetchScalarGridSpec(
             num_scalar_prefetch=1, grid=(width // lanes,),
-            in_specs=[line(), line(), own(), own(), far(), far(), heads(), heads()],
+            in_specs=[line(), line(), own(middle), own(middle), far(), far(), heads(), heads()],
             out_specs=[own(), own()],
             scratch_shapes=[
                 pltpu.VMEM((pairs, 2 * tk, LANE), jnp.bfloat16),
@@ -576,8 +580,12 @@
     shards, owns = refs[:arrays], refs[arrays : arrays + halos]
     fulls = refs[arrays + halos : 2 * arrays + halos]
     windows = refs[2 * arrays + halos : 2 * (arrays + halos)]
-    send, recv, local, halo_send, halo_recv, halo_local = refs[2 * (arrays + halos) :]
+    scratch = refs[2 * (arrays + halos) :]
+    wides, shards = shards, scratch[:arrays]
+    send, recv, local, halo_send, halo_recv, halo_local = scratch[arrays:]
     place = Place(dims)
+    for wide, shard in zip(wides, shards):
+        shard[...] = wide[...].astype(shard.dtype)
     greet(place.peers(), place.me, devices)
     parts = [
         Halo(place, devices, owns[i], windows[i], halo_send.at[i], halo_recv.at[i], halo_local.at[i])
@@ -621,7 +629,7 @@
 
     steps = -(-count // PER_STEP)
     for time in range(steps + 3):
-        for level in (3, 2, 1, 0):
+        for level in GATHER_LEVELS:
             for number in range((time - level) * PER_STEP, (time - level + 1) * PER_STEP):
                 if 0 <= number < count:
                     stage(number, level)
@@ -657,14 +665,14 @@
     anywhere = pl.BlockSpec(memory_space=pl.ANY)
     inside = pl.BlockSpec(memory_space=pltpu.VMEM)
     outs = [
-        jax.ShapeDtypeStruct(shard.shape[:-2] + dims + (2,) + shard.shape[-2:], shard.dtype) for shard in shards
+        jax.ShapeDtypeStruct(shard.shape[:-2] + dims + (2,) + shard.shape[-2:], jnp.bfloat16) for shard in shards
     ] + [jax.ShapeDtypeStruct((5,) + own.shape, own.dtype) for own in owns]
     done = pl.pallas_call(
         functools.partial(gather_kernel, dims, devices, chunks, orders, len(shards), len(owns)),
         in_specs=[inside] * (len(shards) + len(owns)),
         out_specs=[anywhere] * len(outs),
         out_shape=outs,
-        scratch_shapes=[
+        scratch_shapes=[pltpu.VMEM(shard.shape, jnp.bfloat16) for shard in shards] + [
             pltpu.SemaphoreType.DMA((len(chunks), slots)),
             pltpu.SemaphoreType.DMA((len(chunks), slots)),
             pltpu.SemaphoreType.DMA((len(chunks),)),
@@ -678,45 +686,25 @@
     return done[: len(shards)], done[len(shards) :]
 
 
-def halo_kernel(dims, devices, halos, *refs):
-    owns, windows = refs[:halos], refs[halos : 2 * halos]
-    send, recv, local = refs[2 * halos :]
+def scatter_kernel(dims, devices, chunks, arrays, halos, orders, *refs):
+    grads, owns = refs[:arrays], refs[arrays : arrays + halos]
+    outs = refs[arrays + halos : 2 * arrays + halos]
+    windows = refs[2 * arrays + halos : 2 * (arrays + halos)]
+    rest = refs[2 * (arrays + halos) :]
+    count = len(chunks)
+    buffers = [rest[5 * i : 5 * i + 5] for i in range(count)]
+    send, recv, local, halo_send, halo_recv, halo_local = rest[5 * count :]
     place = Place(dims)
-    greet([place.partner], place.me, devices)
-    parts = [Halo(place, devices, owns[i], windows[i], send.at[i], recv.at[i], local.at[i]) for i in range(halos)]
+    if halos:
+        greet(place.peers(), place.me, devices)
+    else:
+        greet(place.peers())
+    parts = [
+        Halo(place, devices, owns[i], windows[i], halo_send.at[i], halo_recv.at[i], halo_local.at[i])
+        for i in range(halos)
+    ]
     for part in parts:
         part.start()
-    for part in parts:
-        part.pass_on()
-    for part in parts:
-        part.finish()
-
-
-def halo(owns, devices):
-    outs = [jax.ShapeDtypeStruct((5,) + own.shape, own.dtype) for own in owns]
-    return pl.pallas_call(
-        functools.partial(halo_kernel, chip_axes(devices), devices, len(owns)),
-        in_specs=[pl.BlockSpec(memory_space=pltpu.VMEM)] * len(owns),
-        out_specs=[pl.BlockSpec(memory_space=pl.ANY)] * len(owns),
-        out_shape=outs,
-        scratch_shapes=[
-            pltpu.SemaphoreType.DMA((len(owns), 4)),
-            pltpu.SemaphoreType.DMA((len(owns), 4)),
-            pltpu.SemaphoreType.DMA((len(owns),)),
-        ],
-        compiler_params=pltpu.CompilerParams(collective_id=1, has_side_effects=True),
-        name="halo",
-    )(*owns)
-
-
-def scatter_kernel(dims, chunks, arrays, orders, *refs):
-    grads, outs = refs[:arrays], refs[arrays : 2 * arrays]
-    rest = refs[2 * arrays :]
-    count = len(chunks)
-    buffers = [rest[5 * i : 5 * i + 5] for i in range(count)]
-    send, recv, local = rest[5 * count :]
-    place = Place(dims)
-    greet(place.peers())
     started = {}
 
     def source(number, core):
@@ -806,8 +794,12 @@
         else:
             add(())
 
-    for time in range(-(-count // PER_STEP) + 4):
-        for level in (4, 3, 2, 1, 0):
+    steps = -(-count // PER_STEP)
+    for time in range(steps + 4):
+        if time == min(SCATTER_PASS, steps + 3):
+            for part in parts:
+                part.pass_on()
+        for level in SCATTER_LEVELS:
             for number in range((time - level) * PER_STEP, (time - level + 1) * PER_STEP):
                 if not 0 <= number < count:
                     continue
@@ -821,9 +813,11 @@
         for level in range(4):
             for copy in started[number, level]:
                 copy.wait_send()
-
-
-def scatter(grads, devices):
+    for part in parts:
+        part.finish()
+
+
+def scatter(grads, owns, devices, orders, identity):
     dims = chip_axes(devices)
     chunks = []
     for array, grad in enumerate(grads):
@@ -834,7 +828,7 @@
             wide = min(lanes, max(CHUNK_BYTES // (2 * rows) // LANE * LANE, LANE))
             wide = max(w for w in range(LANE, wide + 1, LANE) if lanes % w == 0)
             chunks += [(array, None, slice(first, first + wide)) for first in range(0, lanes, wide)]
-    orders = [SCATTER_ORDERS[number % len(SCATTER_ORDERS)] for number in range(len(chunks))]
+    orders = [orders[number % len(orders)] for number in range(len(chunks))]
     scratch = []
     for (array, lead, lanes), order in zip(chunks, orders):
         grad = grads[array]
@@ -847,19 +841,26 @@
             scratch.append(pltpu.VMEM((max(dims[axis] - 1, 1),) + tuple(dims[a] for a in remaining) + piece, grad.dtype))
     slots = 1 + sum(size - 1 for size in dims)
     outs = [jax.ShapeDtypeStruct(grad.shape[:-6] + grad.shape[-2:], jnp.float32) for grad in grads]
-    return pl.pallas_call(
-        functools.partial(scatter_kernel, dims, chunks, len(grads), orders),
-        in_specs=[pl.BlockSpec(memory_space=pl.ANY)] * len(grads),
-        out_specs=[pl.BlockSpec(memory_space=pltpu.VMEM)] * len(grads),
+    outs += [jax.ShapeDtypeStruct((5,) + own.shape, own.dtype) for own in owns]
+    anywhere = pl.BlockSpec(memory_space=pl.ANY)
+    inside = pl.BlockSpec(memory_space=pltpu.VMEM)
+    done = pl.pallas_call(
+        functools.partial(scatter_kernel, dims, devices, chunks, len(grads), len(owns), orders),
+        in_specs=[anywhere] * len(grads) + [inside] * len(owns),
+        out_specs=[inside] * len(grads) + [anywhere] * len(owns),
         out_shape=outs,
         scratch_shapes=scratch + [
             pltpu.SemaphoreType.DMA((len(chunks), slots)),
             pltpu.SemaphoreType.DMA((len(chunks), slots)),
             pltpu.SemaphoreType.DMA((len(chunks),)),
+            pltpu.SemaphoreType.DMA((max(len(owns), 1), 4)),
+            pltpu.SemaphoreType.DMA((max(len(owns), 1), 4)),
+            pltpu.SemaphoreType.DMA((max(len(owns), 1),)),
         ],
-        compiler_params=pltpu.CompilerParams(collective_id=2, has_side_effects=True),
-        name="scatter",
-    )(*grads)
+        compiler_params=pltpu.CompilerParams(collective_id=identity, has_side_effects=True),
+        name="scatter" if not owns else "exchange",
+    )(*grads, *owns)
+    return done[: len(grads)], done[len(grads) :]
 
 
 def adamw_step(master, gradient, first_moment, second_moment):
@@ -902,10 +903,9 @@
     base = reach * rows
     window_first = device * rows - base
     shards = (qkv_weight, out_weight, up_weight, down_weight, vectors)
-    low = [shard.astype(jnp.bfloat16) for shard in shards]
-    vector_part = jnp.pad(low[4].T, ((0, 0), (0, LANE - vectors.shape[0])))
+    vector_part = jnp.pad(vectors.T, ((0, 0), (0, LANE - vectors.shape[0])))
     spans = jnp.pad(jnp.stack([clip_start, clip_end]), ((0, 6), (0, 0)))
-    fulls, (tokens_window, spans_window) = gather(low[:1] + [vector_part] + low[1:4], [tokens, spans], devices)
+    fulls, (tokens_window, spans_window) = gather([qkv_weight, vector_part, out_weight, up_weight, down_weight], [tokens, spans], devices)
     dims = chip_axes(devices)
     qkv_full = fulls[0].reshape(-1, width, width)
     vector_full = fulls[1].reshape(width, LANE)[:, : vectors.shape[0]].T.astype(jnp.float32)
@@ -933,35 +933,36 @@
     needed = jnp.stack([own_start[0] // PROJECT_TILE, (jnp.sum((inside & (starts < base + rows)).astype(jnp.int32)) + jnp.maximum(-window_first, 0) + PROJECT_TILE - 1) // PROJECT_TILE])
 
     query_window, key_window, value_window = project(tokens_window, vector_full, qkv_full, needed, PROJECT_TILE)
-    own = lambda value: lax.slice_in_dim(value, base, base + rows, axis=0)
-    query = own(query_window)
     lower, upper = own_start[:, None], own_end[:, None]
-    mixed, lse = attend(query, key_window, value_window, lower, upper, forward_bounds, tq, tk, GROUP)
+    mixed, lse = attend(query_window, key_window, value_window, lower, upper, forward_bounds, tq, tk, GROUP)
     up_bias = vector_full[8:].reshape(1, -1)
     (result, grad_middle, grad_mixed, delta, grad_out, grad_up, grad_down, middle_rows, bias_row) = middle_block(
         tokens, mixed, cotangent, vector_full, up_bias, out_full, up_full, down_full, MIDDLE_TILE, MIDDLE_CHUNK
     )
     table = jnp.concatenate([lse[:, :heads], delta[:, :heads]], axis=1).T
-    grad_window, table_window = halo([grad_mixed, table], devices)
+    spread = lambda grad, lead=(): grad.reshape(lead + dims + (2, grad.shape[len(lead)] // devices, grad.shape[-1]))
+    (up_owned, down_owned, out_owned), (grad_window, table_window) = scatter(
+        [spread(grad_up), spread(grad_down), spread(grad_out)], [grad_mixed, table], devices, EXCHANGE_ORDERS, 1
+    )
     grad_window = grad_window.reshape(-1, width)
     table_window = table_window.transpose(1, 0, 2).reshape(2 * heads, -1)
     groups = heads // (2 * GROUP)
     lse_window = table_window[:heads].reshape(groups, 2 * GROUP, -1)
     delta_window = table_window[heads:].reshape(groups, 2 * GROUP, -1)
-    grad_query = query_grad(query, grad_mixed, key_window, value_window, lse, delta, lower, upper, query_bounds, rq, rk, GROUP)
+    grad_query = query_grad(query_window, grad_mixed, key_window, value_window, lse, delta, lower, upper, query_bounds, rq, rk, GROUP)
     grad_keys, grad_values = key_grad(
-        own(key_window), own(value_window), query_window, grad_window, lse_window, delta_window,
-        starts[None, :], ends[None, :], key_bounds, base, sk, sq, GROUP,
+        key_window, value_window, query_window, grad_window, lse_window, delta_window,
+        starts[None, :], ends[None, :], key_bounds, base, rows, sk, sq, GROUP,
     )
     grad_tokens, grad_qkv, last_rows = last_block(
         tokens, grad_middle, grad_query, grad_keys, grad_values, vector_full, qkv_full, LAST_TILE
     )
     grad_vectors = jnp.concatenate([last_rows[:4], middle_rows[:4], bias_row.reshape(-1, width)], axis=0)
-    spread = lambda grad, lead=(): grad.reshape(lead + dims + (2, grad.shape[len(lead)] // devices, grad.shape[-1]))
     vector_rows = grad_vectors.reshape(vectors.shape[0], devices, -1).transpose(1, 0, 2).reshape(devices, -1)
     vector_rows = jnp.pad(vector_rows, ((0, 0), (0, 8 * LANE - vector_rows.shape[1]))).reshape(dims + (2, 8, LANE))
-    owned = scatter([spread(grad_up), spread(grad_down), spread(grad_out), spread(grad_qkv, (3,)), vector_rows], devices)
-    owned = (owned[3], owned[2], owned[0], owned[1], owned[4].reshape(-1)[: vectors.size].reshape(vectors.shape))
+    (qkv_owned, vector_owned), _ = scatter([spread(grad_qkv, (3,)), vector_rows], [], devices, SCATTER_ORDERS, 2)
+    vector_owned = vector_owned.reshape(-1)[: vectors.size].reshape(vectors.shape)
+    owned = (qkv_owned, out_owned, up_owned, down_owned, vector_owned)
     firsts = (qkv_first, out_first, up_first, down_first, vector_first)
     seconds = (qkv_second, out_second, up_second, down_second, vector_second)
     stepped = [adamw_step(*four) for four in zip(shards, owned, firsts, seconds)]

time: 560 us -> 531 us (0.948)
  Pallas kernels: 511 us -> 496 us
  other arithmetic: 18.7 us -> 11.3 us
  local copies, waits for them, and re-layouts: 23.7 us -> 18 us
    pallas_call x2, Pallas kernels: 182 us -> 170 us  [scatter(): pl.pallas_call(functools.partial(scatter_kernel, dims, devices, chunks, l...]
    convert_element_type x5 -> x0, other arithmetic: 7.08 us -> none  [per_device(): low = [shard.astype(jnp.bfloat16) for shard in shards]]
    slice x4 -> x1, local copies, waits for them, and re-layouts: 7.15 us -> 0.73 us  [per_device(): vector_owned.reshape(-1)[:vectors.size].reshape(vectors.shape)]
where the time goes in v3:
time: 531 us; the launch traced here: 529 us
  Pallas kernels  496 us (93%)
  local copies, waits for them, and re-layouts  18 us (3%)
  other arithmetic  11.3 us (2%)
    pallas_call x2, Pallas kernels, scatter(): pl.pallas_call(functools.partial(scatter_kernel, dims, devices, chunks, l...  170 us
    pallas_call x1, Pallas kernels, gather(): pl.pallas_call(functools.partial(gather_kernel, dims, devices, chunks, or...  124 us
    pallas_call x1, Pallas kernels, query_grad(): pl.pallas_call(functools.partial(query_grad_kernel, tq, tk, pairs), grid_...  49.8 us
    pallas_call x1, Pallas kernels, key_grad(): pl.pallas_call(functools.partial(key_grad_kernel, tk, tq, pairs, base), g...  45.7 us
    pallas_call x1, Pallas kernels, attend(): pl.pallas_call(functools.partial(forward_kernel, tq, tk, pairs), grid_spe...  42.2 us
    pallas_call x1, Pallas kernels, middle_block(): pl.pallas_call(functools.partial(middle_kernel, tile), grid=(hidden // ch...  35.9 us
    pallas_call x1, Pallas kernels, project(): pl.pallas_call(functools.partial(project_kernel, tile), grid_spec=pltpu.P...  15.5 us
    pallas_call x1, Pallas kernels, last_block(): pl.pallas_call(functools.partial(last_kernel, tile), out_shape=[jax.Shape...  12.1 us

profile of v3, /device:TPU:0, one launch (start us, length us, event | category | flops | bytes accessed | tf_op | source)
XLA Modules:
  0.0 528.8 jit_solution(3759706164266173002)
XLA Ops:
  2.7 0.8 copy.62
  4.0 124.5 %gather.1 = (bf16[3,4,2,2,2,24,768]{6,5,4,3,2,1,0:T(8,128)(2,1)}, bf16[4,2,2,2,24,128]{5,4,3,2,1,0:T(8,128)(2,1)}, bf16[4,2,2,2,24,768]{5,4,3,2,1,0:T(8,128)(2,1...) custom-call(f32[3,24,768]{2,1,0:T(8,128)} %refs_0_.1, ...), custom_call_target="tpu_custom_call" | custom-call | tf_op jit(solution)/shard_map/gather/pallas_call | solution.py:670
  128.5 1.7 fusion.14
  134.7 1.0 copy.76
  136.4 15.5 %project.1 = (bf16[3840,768]{1,0:T(8,128)(2,1)}, bf16[3840,768]{1,0:T(8,128)(2,1)}, bf16[3840,768]{1,0:T(8,128)(2,1)}) custom-call(s32[2]{0:T(128)} %pad_add_fusion.4.active, bf16[3840,768]{1,0:T(8,128)(2,1)} %bitcast.48, f32[12,768]{1,0:T(8,128)} %convert_bitcast_fusion.vectors, bf16[3,768,768]{2,1,0:T(8,128)(2,1)} %bitcast.46), custom_call_target="tpu_custom_call" | custom-call | tf_op jit(solution)/shard_map/project/pallas_call | solution.py:332
  152.8 0.9 broadcast_in_dim.26.lower
  153.7 0.9 broadcast_in_dim.27.upper
  154.7 42.2 %attend.1 = (bf16[768,768]{1,0:T(8,128)(2,1)}, f32[768,128]{1,0:T(8,128)}) custom-call(s32[6]{0:T(128)} %reshape.204.bounds, s32[768,1]{1,0:T(8,128)} %broadcast_in_dim.26.lower, s32[768,1]{1,0:T(8,128)} %broadcast_in_dim.27.upper, bf16[3840,768]{1,0:T(8,128)(2,1)} %get-tuple-element.54.q_ref, bf16[3840,768]{1,0:T(8,128)(2,1)} %get-tuple-element.55.k_ref, ...), custom_call_target="tpu_custom_call" | custom-call | tf_op jit(solution)/shard_map/attend/pallas_call | solution.py:132
  196.9 0.7 slice_bitcast_fusion
  198.3 35.9 %middle.1 = (bf16[768,768]{1,0:T(8,128)(2,1)}, f32[768,768]{1,0:T(8,128)}, bf16[768,768]{1,0:T(8,128)(2,1)}, f32[768,128]{1,0:T(8,128)}, bf16[768,768]{1,0:T(8,1...) custom-call(bf16[768,768]{1,0:T(8,128)(2,1)} %tokens.3, ...), custom_call_target="tpu_custom_call" | custom-call | tf_op jit(solution)/shard_map/middle/pallas_call | solution.py:429
  234.1 1.2 copy.71
  236.2 115.9 %exchange.1 = (f32[24,3072]{1,0:T(8,128)}, f32[96,768]{1,0:T(8,128)}, f32[24,768]{1,0:T(8,128)}, bf16[5,768,768]{2,1,0:T(8,128)(2,1)}, f32[5,24,768]{2,1,0:T(8,128)}) custom-call(bf16[4,2,2,2,24,3072]{5,4,3,2,1,0:T(8,128)(2,1)} %bitcast.50, bf16[4,2,2,2,96,768]{5,4,3,2,1,0:T(8,128)(2,1)} %bitcast.51, bf16[4,2,2,2,24,768]{5,4,3,2,1,0:T(8,128)(2,1)} %bitcast.56, ...), custom_call_target="tpu_custom_call" | custom-call | tf_op jit(solution)/shard_map/exchange/pallas_call | solution.py:847
  352.0 1.1 fusion.20
  353.3 0.8 reshape.218.lse_ref
  354.2 0.8 reshape.219.delta_ref
  356.6 45.7 %key_grad.1 = (bf16[768,768]{1,0:T(8,128)(2,1)}, bf16[768,768]{1,0:T(8,128)(2,1)}) custom-call(s32[6]{0:T(128)} %reshape.213.bounds, s32[1,3840]{1,0:T(1,128)} %get-tuple-element.110.lower, s32[1,3840]{1,0:T(1,128)} %get-tuple-element.111.upper, bf16[3840,768]{1,0:T(8,128)(2,1)} %get-tuple-element.55.k_ref, bf16[3840,768]{1,0:T(8,128)(2,1)} %get-tuple-element.56.v_ref, ...), custom_call_target="tpu_custom_call" | custom-call | tf_op jit(solution)/shard_map/key_grad/pallas_call | solution.py:271
  402.9 49.8 %query_grad.1.grad_query = bf16[768,768]{1,0:T(8,128)(2,1)} custom-call(s32[6]{0:T(128)} %reshape.212.bounds, s32[768,1]{1,0:T(8,128)} %broadcast_in_dim.26.lower, s32[768,1]{1,0:T(8,128)} %broadcast_in_dim.27.upper, bf16[3840,768]{1,0:T(8,128)(2,1)} %get-tuple-element.54.q_ref, bf16[768,768]{1,0:T(8,128)(2,1)} %get-tuple-element.63.g_ref.refs_3_, ...), custom_call_target="tpu_custom_call" | custom-call | tf_op jit(solution)/shard_map/query_grad/pallas_call | solution.py:202
  452.8 12.1 %last.1 = (f32[768,768]{1,0:T(8,128)}, bf16[3,768,768]{2,1,0:T(8,128)(2,1)}, f32[8,768]{1,0:T(8,128)}) custom-call(bf16[768,768]{1,0:T(8,128)(2,1)} %tokens.3, f32[768,768]{1,0:T(8,128)} %get-tuple-element.62.grad_middle, bf16[768,768]{1,0:T(8,128)(2,1)} %query_grad.1.grad_query, bf16[768,768]{1,0:T(8,128)(2,1)} %get-tuple-element.71.grad_keys, ...), custom_call_target="tpu_custom_call" | custom-call | tf_op jit(solution)/shard_map/last/pallas_call | solution.py:481
  464.8 0.7 slice.64
  468.1 54.4 %scatter.1 = (f32[3,24,768]{2,1,0:T(8,128)}, f32[8,128]{1,0:T(8,128)}) custom-call(bf16[3,4,2,2,2,24,768]{6,5,4,3,2,1,0:T(8,128)(2,1)} %bitcast.54, f32[4,2,2,2,8,128]{5,4,3,2,1,0:T(8,128)} %bitcast.59), custom_call_target="tpu_custom_call" | custom-call | tf_op jit(solution)/shard_map/scatter/pallas_call | solution.py:847
  522.6 1.9 add_multiply_fusion.2
  524.5 0.7 slice.66
  526.0 1.0 add_multiply_fusion
  527.1 1.0 add_multiply_fusion.1
  (91 shorter events, 13.9 us)
Async XLA Ops:
  198.3 37.1 %copy-start = (f32[768,128]{1,0:T(8,128)S(1)}, f32[768,128]{1,0:T(8,128)}, u32[]{:S(2)}) copy-start(f32[768,128]{1,0:T(8,128)} %get-tuple-element.64.lse_ref) | copy-start | bytes 1179652
  452.8 13.4 %copy-start.17 = (f32[1,3072]{1,0:T(1,128)S(1)}, f32[1,3072]{1,0:T(1,128)}, u32[]{:S(2)}) copy-start(f32[1,3072]{1,0:T(1,128)} %get-tuple-element.77) | copy-start | bytes 36868
  452.8 14.2 %copy-start.20 = (f32[8,768]{1,0:T(8,128)S(1)}, f32[8,768]{1,0:T(8,128)}, u32[]{:S(2)}) copy-start(f32[8,768]{1,0:T(8,128)} %get-tuple-element.76) | copy-start | bytes 73732
  467.1 55.4 %copy-start.3 = (f32[3,24,768]{2,1,0:T(8,128)S(1)}, f32[3,24,768]{2,1,0:T(8,128)}, u32[]{:S(2)}) copy-start(f32[3,24,768]{2,1,0:T(8,128)} %refs_0_.1) | copy-start | bytes 663556
  467.1 55.4 %copy-start.11 = (f32[3,24,768]{2,1,0:T(8,128)S(1)}, f32[3,24,768]{2,1,0:T(8,128)}, u32[]{:S(2)}) copy-start(f32[3,24,768]{2,1,0:T(8,128)} %param.28) | copy-start | bytes 663556
  467.1 55.4 %copy-start.12 = (f32[3,24,768]{2,1,0:T(8,128)S(1)}, f32[3,24,768]{2,1,0:T(8,128)}, u32[]{:S(2)}) copy-start(f32[3,24,768]{2,1,0:T(8,128)} %param.33) | copy-start | bytes 663556
  468.1 57.3 %copy-start.16 = (f32[12,24]{1,0:T(8,128)S(1)}, f32[12,24]{1,0:T(8,128)}, u32[]{:S(2)}) copy-start(f32[12,24]{1,0:T(8,128)} %param.27) | copy-start | bytes 3460
  468.1 57.3 %copy-start.18 = (f32[12,24]{1,0:T(8,128)S(1)}, f32[12,24]{1,0:T(8,128)}, u32[]{:S(2)}) copy-start(f32[12,24]{1,0:T(8,128)} %param.32) | copy-start | bytes 3460
  468.1 57.3 %copy-start.19 = (f32[12,24]{1,0:T(8,128)S(1)}, f32[12,24]{1,0:T(8,128)}, u32[]{:S(2)}) copy-start(f32[12,24]{1,0:T(8,128)} %param.37) | copy-start | bytes 3460
  468.1 57.9 %copy-start.1 = (f32[96,768]{1,0:T(8,128)S(1)}, f32[96,768]{1,0:T(8,128)}, u32[]{:S(2)}) copy-start(f32[96,768]{1,0:T(8,128)} %refs_4_.1) | copy-start | bytes 884740
  468.1 57.9 %copy-start.5 = (f32[96,768]{1,0:T(8,128)S(1)}, f32[96,768]{1,0:T(8,128)}, u32[]{:S(2)}) copy-start(f32[96,768]{1,0:T(8,128)} %param.31) | copy-start | bytes 884740
  468.1 57.9 %copy-start.6 = (f32[96,768]{1,0:T(8,128)S(1)}, f32[96,768]{1,0:T(8,128)}, u32[]{:S(2)}) copy-start(f32[96,768]{1,0:T(8,128)} %param.36) | copy-start | bytes 884740
  468.1 57.9 %copy-start.10 = (f32[96,768]{1,0:T(8,128)S(1)}, f32[96,768]{1,0:T(8,128)}, u32[]{:S(2)}) copy-start(f32[96,768]{1,0:T(8,128)} %get-tuple-element.81) | copy-start | bytes 884740
  522.5 4.6 copy-start.2
  522.5 4.6 copy-start.7
  522.5 4.5 copy-start.8
  522.5 4.5 copy-start.9
  524.5 3.6 copy-start.4
  524.5 3.6 copy-start.13
  524.5 3.6 copy-start.14
  524.5 3.6 copy-start.15

commit v4 on v3

--- a/solution.py
+++ b/solution.py
@@ -23,14 +23,14 @@
 adam_eps = 1e-08
 norm_eps = 1e-05
 masked_score = -1e30
-FORWARD_TILES = (256, 384)
+FORWARD_TILES = (256, 256)
 QUERY_TILES = (256, 256)
 KEY_TILES = (256, 256)
 PROJECT_TILE = 768
 MIDDLE_TILE = 256
 MIDDLE_CHUNK = 512
 LAST_TILE = 256
-GROUP = 2
+GROUP = 3
 CHUNK_BYTES = 40000
 PER_STEP = 4
 HALO_START = 0
@@ -69,124 +69,114 @@
     return jnp.where(lane < HD, both[:rows], both[rows:])
 
 
-def column(table, place):
-    lane = lax.broadcasted_iota(jnp.int32, table.shape, 1)
-    return jnp.sum(jnp.where(lane == place, table, 0.0), axis=1, keepdims=True)
-
-
-def forward_kernel(tq, tk, pairs, bounds, lower, upper, q_ref, k_ref, v_ref, o_ref, lse_ref, qs, peak, acc):
-    group = pl.program_id(0)
+def joined(turned):
+    rows = turned.shape[1] // 2
+    return jnp.concatenate([turned[:HD, :rows], turned[HD:, rows:]], axis=0).T
+
+
+def forward_kernel(tq, tk, pairs, bounds, lower, upper, q_ref, k_ref, v_ref, o_ref, lse_ref, qs, peak, total, acc):
     tiles = q_ref.shape[0] // tq
-    ones = jnp.ones((tk, LANE), jnp.bfloat16)
-
-    @pl.when(group == 0)
-    def _():
-        lse_ref[...] = jnp.zeros_like(lse_ref)
 
     def one_tile(tile, none):
         rows = pl.ds(pl.multiple_of(tile * tq, tq), tq)
         for pair in range(pairs):
             qs[pair] = stacked(q_ref[rows, pair * LANE : (pair + 1) * LANE], HD ** -0.5)
         peak[...] = jnp.full_like(peak, masked_score)
+        total[...] = jnp.zeros_like(total)
         acc[...] = jnp.zeros_like(acc)
-        low, high = lower[rows, :], upper[rows, :]
+        low, high = lower[:, rows], upper[:, rows]
 
         def step(key_tile, none):
             first = pl.multiple_of(key_tile * tk, tk)
-            places = first + lax.broadcasted_iota(jnp.int32, (tq, tk), 1)
+            places = first + lax.broadcasted_iota(jnp.int32, (tk, tq), 0)
             bias = jnp.where((places >= low) & (places < high), 0.0, masked_score)
-            bias = jnp.concatenate([bias, bias], axis=0)
+            bias = jnp.concatenate([bias, bias], axis=1)
             for pair in range(pairs):
                 lanes = slice(pair * LANE, (pair + 1) * LANE)
-                scores = dot(qs[pair], k_ref[pl.ds(first, tk), lanes], NT) + bias
+                scores = dot(k_ref[pl.ds(first, tk), lanes], qs[pair], NT) + bias
                 old = peak[pair]
-                new = jnp.maximum(old, jnp.max(scores, axis=1, keepdims=True))
+                new = jnp.maximum(old, jnp.max(scores, axis=0, keepdims=True))
                 peak[pair] = new
-                weights = jnp.exp(scores - jnp.concatenate([new] * (tk // LANE), axis=1)).astype(jnp.bfloat16)
-                values = jnp.concatenate([v_ref[pl.ds(first, tk), lanes], ones], axis=1)
+                weights = jnp.exp(scores - new)
                 scale = jnp.exp(old - new)
-                acc[pair] = acc[pair] * jnp.concatenate([scale, scale], axis=1) + dot(weights, values)
+                total[pair] = total[pair] * scale + jnp.sum(weights, axis=0, keepdims=True)
+                acc[pair] = acc[pair] * scale + dot(v_ref[pl.ds(first, tk), lanes].T, weights.astype(jnp.bfloat16))
             return none
 
         lax.fori_loop(bounds[2 * tile], bounds[2 * tile + 1], step, 0)
-        lane = lax.broadcasted_iota(jnp.int32, (tq, LANE), 1)
-        table = lse_ref[rows, :]
         for pair in range(pairs):
-            both = acc[pair]
-            total = both[:, LANE:]
-            o_ref[rows, pair * LANE : (pair + 1) * LANE] = unstacked(both[:, :LANE] / total).astype(o_ref.dtype)
-            logs = peak[pair] + jnp.log(total)
-            head = (group * pairs + pair) * 2
-            table = jnp.where(lane == head, logs[:tq], table)
-            table = jnp.where(lane == head + 1, logs[tq:], table)
-        lse_ref[rows, :] = table
+            o_ref[rows, pair * LANE : (pair + 1) * LANE] = joined(acc[pair] / total[pair]).astype(o_ref.dtype)
+            logs = peak[pair] + jnp.log(total[pair])
+            lse_ref[0, 2 * pair : 2 * pair + 1, rows] = logs[:, :tq]
+            lse_ref[0, 2 * pair + 1 : 2 * pair + 2, rows] = logs[:, tq:]
         return none
 
     lax.fori_loop(0, tiles, one_tile, 0)
 
 
 def attend(query, keys, values, lower, upper, bounds, tq, tk, pairs):
-    rows, (window, width) = lower.shape[0], keys.shape
+    rows, (window, width) = lower.shape[1], keys.shape
     middle = window // rows // 2
     lanes = pairs * LANE
+    far = lambda: pl.BlockSpec((window, lanes), lambda g, b: (0, g))
+    line = lambda: pl.BlockSpec((1, rows), lambda g, b: (0, 0))
     return pl.pallas_call(
         functools.partial(forward_kernel, tq, tk, pairs),
         grid_spec=pltpu.PrefetchScalarGridSpec(
             num_scalar_prefetch=1, grid=(width // lanes,),
-            in_specs=[
-                pl.BlockSpec((rows, 1), lambda g, b: (0, 0)),
-                pl.BlockSpec((rows, 1), lambda g, b: (0, 0)),
-                pl.BlockSpec((rows, lanes), lambda g, b: (middle, g)),
-                pl.BlockSpec((window, lanes), lambda g, b: (0, g)),
-                pl.BlockSpec((window, lanes), lambda g, b: (0, g)),
+            in_specs=[line(), line(), pl.BlockSpec((rows, lanes), lambda g, b: (middle, g)), far(), far()],
+            out_specs=[
+                pl.BlockSpec((rows, lanes), lambda g, b: (0, g)),
+                pl.BlockSpec((1, 2 * pairs, rows), lambda g, b: (g, 0, 0)),
             ],
-            out_specs=[pl.BlockSpec((rows, lanes), lambda g, b: (0, g)), pl.BlockSpec((rows, LANE), lambda g, b: (0, 0))],
             scratch_shapes=[
                 pltpu.VMEM((pairs, 2 * tq, LANE), jnp.bfloat16),
-                pltpu.VMEM((pairs, 2 * tq, LANE), jnp.float32),
-                pltpu.VMEM((pairs, 2 * tq, 2 * LANE), jnp.float32),
+                pltpu.VMEM((pairs, 1, 2 * tq), jnp.float32),
+                pltpu.VMEM((pairs, 1, 2 * tq), jnp.float32),
+                pltpu.VMEM((pairs, LANE, 2 * tq), jnp.float32),
             ],
         ),
-        out_shape=[jax.ShapeDtypeStruct((rows, width), jnp.bfloat16), jax.ShapeDtypeStruct((rows, LANE), jnp.float32)],
+        out_shape=[
+            jax.ShapeDtypeStruct((rows, width), jnp.bfloat16),
+            jax.ShapeDtypeStruct((width // lanes, 2 * pairs, rows), jnp.float32),
+        ],
         name="attend",
     )(bounds, lower, upper, query, keys, values)
 
 
-def query_grad_kernel(tq, tk, pairs, bounds, lower, upper, q_ref, g_ref, k_ref, v_ref, lse_ref, delta_ref, dq_ref, qs, gs, logs, deltas, acc):
-    group = pl.program_id(0)
+def query_grad_kernel(tq, tk, pairs, bounds, lower, upper, q_ref, g_ref, k_ref, v_ref, lse_ref, delta_ref, dq_ref, qs, gs, acc):
     tiles = q_ref.shape[0] // tq
 
     def one_tile(tile, none):
         rows = pl.ds(pl.multiple_of(tile * tq, tq), tq)
-        table, other = lse_ref[rows, :], delta_ref[rows, :]
+        logs, deltas = [], []
         for pair in range(pairs):
             lanes = slice(pair * LANE, (pair + 1) * LANE)
             qs[pair] = stacked(q_ref[rows, lanes], HD ** -0.5)
             gs[pair] = stacked(g_ref[rows, lanes], None)
-            head = (group * pairs + pair) * 2
-            logs[pair] = jnp.broadcast_to(jnp.concatenate([column(table, head), column(table, head + 1)], axis=0), logs.shape[1:])
-            deltas[pair] = jnp.broadcast_to(jnp.concatenate([column(other, head), column(other, head + 1)], axis=0), logs.shape[1:])
+            for held, ref in ((logs, lse_ref), (deltas, delta_ref)):
+                halves = [ref[0, 2 * pair + half : 2 * pair + half + 1, rows] for half in range(2)]
+                held.append(jnp.concatenate(halves, axis=1))
         acc[...] = jnp.zeros_like(acc)
-        low, high = lower[rows, :], upper[rows, :]
+        low, high = lower[:, rows], upper[:, rows]
 
         def step(key_tile, none):
             first = pl.multiple_of(key_tile * tk, tk)
-            places = first + lax.broadcasted_iota(jnp.int32, (tq, tk), 1)
+            places = first + lax.broadcasted_iota(jnp.int32, (tk, tq), 0)
             bias = jnp.where((places >= low) & (places < high), 0.0, masked_score)
-            bias = jnp.concatenate([bias, bias], axis=0)
+            bias = jnp.concatenate([bias, bias], axis=1)
             for pair in range(pairs):
                 lanes = slice(pair * LANE, (pair + 1) * LANE)
                 keys = k_ref[pl.ds(first, tk), lanes]
-                scores = dot(qs[pair], keys, NT) + bias
-                probs = jnp.exp(scores - jnp.concatenate([logs[pair]] * (tk // LANE), axis=1))
-                grad_probs = dot(gs[pair], v_ref[pl.ds(first, tk), lanes], NT)
-                grad_scores = (probs * (grad_probs - jnp.concatenate([deltas[pair]] * (tk // LANE), axis=1))).astype(jnp.bfloat16)
-                acc[pair] += dot(grad_scores, keys)
+                probs = jnp.exp(dot(keys, qs[pair], NT) + bias - logs[pair])
+                grad_probs = dot(v_ref[pl.ds(first, tk), lanes], gs[pair], NT)
+                grad_scores = (probs * (grad_probs - deltas[pair])).astype(jnp.bfloat16)
+                acc[pair] += dot(keys.T, grad_scores)
             return none
 
         lax.fori_loop(bounds[2 * tile], bounds[2 * tile + 1], step, 0)
         for pair in range(pairs):
-            dq_ref[rows, pair * LANE : (pair + 1) * LANE] = (unstacked(acc[pair]) * HD ** -0.5).astype(dq_ref.dtype)
+            dq_ref[rows, pair * LANE : (pair + 1) * LANE] = joined(acc[pair] * HD ** -0.5).astype(dq_ref.dtype)
         return none
 
     lax.fori_loop(0, tiles, one_tile, 0)
@@ -198,19 +188,18 @@
     lanes = pairs * LANE
     own = lambda at=0: pl.BlockSpec((rows, lanes), lambda g, b: (at, g))
     far = lambda: pl.BlockSpec((window, lanes), lambda g, b: (0, g))
-    fixed = lambda cols: pl.BlockSpec((rows, cols), lambda g, b: (0, 0))
+    line = lambda: pl.BlockSpec((1, rows), lambda g, b: (0, 0))
+    heads = lambda: pl.BlockSpec((1, 2 * pairs, rows), lambda g, b: (g, 0, 0))
     return pl.pallas_call(
         functools.partial(query_grad_kernel, tq, tk, pairs),
         grid_spec=pltpu.PrefetchScalarGridSpec(
             num_scalar_prefetch=1, grid=(width // lanes,),
-            in_specs=[fixed(1), fixed(1), own(middle), own(), far(), far(), fixed(LANE), fixed(LANE)],
+            in_specs=[line(), line(), own(middle), own(), far(), far(), heads(), heads()],
             out_specs=own(),
             scratch_shapes=[
                 pltpu.VMEM((pairs, 2 * tq, LANE), jnp.bfloat16),
                 pltpu.VMEM((pairs, 2 * tq, LANE), jnp.bfloat16),
-                pltpu.VMEM((pairs, 2 * tq, LANE), jnp.float32),
-                pltpu.VMEM((pairs, 2 * tq, LANE), jnp.float32),
-                pltpu.VMEM((pairs, 2 * tq, LANE), jnp.float32),
+                pltpu.VMEM((pairs, LANE, 2 * tq), jnp.float32),
             ],
         ),
         out_shape=jax.ShapeDtypeStruct((rows, width), jnp.bfloat16),
@@ -933,13 +922,14 @@
     needed = jnp.stack([own_start[0] // PROJECT_TILE, (jnp.sum((inside & (starts < base + rows)).astype(jnp.int32)) + jnp.maximum(-window_first, 0) + PROJECT_TILE - 1) // PROJECT_TILE])
 
     query_window, key_window, value_window = project(tokens_window, vector_full, qkv_full, needed, PROJECT_TILE)
-    lower, upper = own_start[:, None], own_end[:, None]
+    lower, upper = own_start[None, :], own_end[None, :]
     mixed, lse = attend(query_window, key_window, value_window, lower, upper, forward_bounds, tq, tk, GROUP)
     up_bias = vector_full[8:].reshape(1, -1)
     (result, grad_middle, grad_mixed, delta, grad_out, grad_up, grad_down, middle_rows, bias_row) = middle_block(
         tokens, mixed, cotangent, vector_full, up_bias, out_full, up_full, down_full, MIDDLE_TILE, MIDDLE_CHUNK
     )
-    table = jnp.concatenate([lse[:, :heads], delta[:, :heads]], axis=1).T
+    delta = delta[:, :heads].T
+    table = jnp.concatenate([lse.reshape(heads, rows), delta], axis=0)
     spread = lambda grad, lead=(): grad.reshape(lead + dims + (2, grad.shape[len(lead)] // devices, grad.shape[-1]))
     (up_owned, down_owned, out_owned), (grad_window, table_window) = scatter(
         [spread(grad_up), spread(grad_down), spread(grad_out)], [grad_mixed, table], devices, EXCHANGE_ORDERS, 1
@@ -949,7 +939,7 @@
     groups = heads // (2 * GROUP)
     lse_window = table_window[:heads].reshape(groups, 2 * GROUP, -1)
     delta_window = table_window[heads:].reshape(groups, 2 * GROUP, -1)
-    grad_query = query_grad(query_window, grad_mixed, key_window, value_window, lse, delta, lower, upper, query_bounds, rq, rk, GROUP)
+    grad_query = query_grad(query_window, grad_mixed, key_window, value_window, lse, delta.reshape(lse.shape), lower, upper, query_bounds, rq, rk, GROUP)
     grad_keys, grad_values = key_grad(
         key_window, value_window, query_window, grad_window, lse_window, delta_window,
         starts[None, :], ends[None, :], key_bounds, base, rows, sk, sq, GROUP,

time: 531 us -> 535 us (level); the launches traced: 529 us -> 540 us
  Pallas kernels: 496 us -> 508 us
    pallas_call x2, Pallas kernels: 170 us -> 180 us  [scatter(): pl.pallas_call(functools.partial(scatter_kernel, dims, devices, chunks, l...]
    pallas_call x1, Pallas kernels: 42.2 us -> 49.7 us  [attend(): pl.pallas_call(functools.partial(forward_kernel, tq, tk, pairs), grid_spe...]
where the time goes in v4:
time: 535 us; the launch traced here: 540 us
  Pallas kernels  508 us (95%)
  local copies, waits for them, and re-layouts  17.1 us (3%)
  other arithmetic  11.3 us (2%)
    pallas_call x2, Pallas kernels, scatter(): pl.pallas_call(functools.partial(scatter_kernel, dims, devices, chunks, l...  180 us
    pallas_call x1, Pallas kernels, gather(): pl.pallas_call(functools.partial(gather_kernel, dims, devices, chunks, or...  124 us
    pallas_call x1, Pallas kernels, attend(): pl.pallas_call(functools.partial(forward_kernel, tq, tk, pairs), grid_spe...  49.7 us
    pallas_call x1, Pallas kernels, query_grad(): pl.pallas_call(functools.partial(query_grad_kernel, tq, tk, pairs), grid_...  46.8 us
    pallas_call x1, Pallas kernels, key_grad(): pl.pallas_call(functools.partial(key_grad_kernel, tk, tq, pairs, base), g...  44.3 us
    pallas_call x1, Pallas kernels, middle_block(): pl.pallas_call(functools.partial(middle_kernel, tile), grid=(hidden // ch...  35.9 us
    pallas_call x1, Pallas kernels, project(): pl.pallas_call(functools.partial(project_kernel, tile), grid_spec=pltpu.P...  15.4 us
    pallas_call x1, Pallas kernels, last_block(): pl.pallas_call(functools.partial(last_kernel, tile), out_shape=[jax.Shape...  12.1 us

profile of v4, /device:TPU:0, one launch (start us, length us, event | category | flops | bytes accessed | tf_op | source)
XLA Modules:
  0.0 540.4 jit_solution(15496551921733444820)
XLA Ops:
  2.7 0.8 copy.54
  4.0 124.5 %gather.1 = (bf16[3,4,2,2,2,24,768]{6,5,4,3,2,1,0:T(8,128)(2,1)}, bf16[4,2,2,2,24,128]{5,4,3,2,1,0:T(8,128)(2,1)}, bf16[4,2,2,2,24,768]{5,4,3,2,1,0:T(8,128)(2,1...) custom-call(f32[3,24,768]{2,1,0:T(8,128)} %refs_0_.1, ...), custom_call_target="tpu_custom_call" | custom-call | tf_op jit(solution)/shard_map/gather/pallas_call | solution.py:659
  128.5 1.7 fusion.12
  130.9 0.7 broadcast_subtract_fusion
  134.7 1.0 copy.62
  136.4 15.4 %project.1 = (bf16[3840,768]{1,0:T(8,128)(2,1)}, bf16[3840,768]{1,0:T(8,128)(2,1)}, bf16[3840,768]{1,0:T(8,128)(2,1)}) custom-call(s32[2]{0:T(128)} %pad_add_fusion.3.active, bf16[3840,768]{1,0:T(8,128)(2,1)} %bitcast.45, f32[12,768]{1,0:T(8,128)} %convert_bitcast_fusion.vectors, bf16[3,768,768]{2,1,0:T(8,128)(2,1)} %bitcast.43), custom_call_target="tpu_custom_call" | custom-call | tf_op jit(solution)/shard_map/project/pallas_call | solution.py:321
  154.2 49.7 %attend.1 = (bf16[768,768]{1,0:T(8,128)(2,1)}, f32[2,6,768]{2,1,0:T(8,128)}) custom-call(s32[6]{0:T(128)} %reshape.208.bounds, s32[1,768]{1,0:T(1,128)} %broadcast_in_dim.21.lower, s32[1,768]{1,0:T(1,128)} %broadcast_in_dim.22.upper, bf16[3840,768]{1,0:T(8,128)(2,1)} %get-tuple-element.54.q_ref, bf16[3840,768]{1,0:T(8,128)(2,1)} %get-tuple-element.55.k_ref, ...), custom_call_target="tpu_custom_call" | custom-call | tf_op jit(solution)/shard_map/attend/pallas_call | solution.py:123
  203.9 0.7 slice_bitcast_fusion.1
  205.2 35.9 %middle.1 = (bf16[768,768]{1,0:T(8,128)(2,1)}, f32[768,768]{1,0:T(8,128)}, bf16[768,768]{1,0:T(8,128)(2,1)}, f32[768,128]{1,0:T(8,128)}, bf16[768,768]{1,0:T(8,1...) custom-call(bf16[768,768]{1,0:T(8,128)(2,1)} %tokens.3, ...), custom_call_target="tpu_custom_call" | custom-call | tf_op jit(solution)/shard_map/middle/pallas_call | solution.py:418
  241.1 1.2 copy.56
  243.0 121.4 %exchange.1 = (f32[24,3072]{1,0:T(8,128)}, f32[96,768]{1,0:T(8,128)}, f32[24,768]{1,0:T(8,128)}, bf16[5,768,768]{2,1,0:T(8,128)(2,1)}, f32[5,24,768]{2,1,0:T(8,128)}) custom-call(bf16[4,2,2,2,24,3072]{5,4,3,2,1,0:T(8,128)(2,1)} %bitcast.47, bf16[4,2,2,2,96,768]{5,4,3,2,1,0:T(8,128)(2,1)} %bitcast.48, bf16[4,2,2,2,24,768]{5,4,3,2,1,0:T(8,128)(2,1)} %bitcast.53, ...), custom_call_target="tpu_custom_call" | custom-call | tf_op jit(solution)/shard_map/exchange/pallas_call | solution.py:836
  364.4 1.1 fusion.18
  365.6 0.8 reshape.223.lse_ref
  366.5 0.8 reshape.224.delta_ref
  368.6 44.3 %key_grad.1 = (bf16[768,768]{1,0:T(8,128)(2,1)}, bf16[768,768]{1,0:T(8,128)(2,1)}) custom-call(s32[6]{0:T(128)} %reshape.217.bounds, s32[1,3840]{1,0:T(1,128)} %get-tuple-element.106.lower, s32[1,3840]{1,0:T(1,128)} %get-tuple-element.107.upper, bf16[3840,768]{1,0:T(8,128)(2,1)} %get-tuple-element.55.k_ref, bf16[3840,768]{1,0:T(8,128)(2,1)} %get-tuple-element.56.v_ref, ...), custom_call_target="tpu_custom_call" | custom-call | tf_op jit(solution)/shard_map/key_grad/pallas_call | solution.py:260
  413.5 46.8 %query_grad.1.grad_query = bf16[768,768]{1,0:T(8,128)(2,1)} custom-call(s32[6]{0:T(128)} %reshape.208.bounds, s32[1,768]{1,0:T(1,128)} %broadcast_in_dim.21.lower, s32[1,768]{1,0:T(1,128)} %broadcast_in_dim.22.upper, bf16[3840,768]{1,0:T(8,128)(2,1)} %get-tuple-element.54.q_ref, bf16[768,768]{1,0:T(8,128)(2,1)} %get-tuple-element.63.g_ref.refs_3_, ...), custom_call_target="tpu_custom_call" | custom-call | tf_op jit(solution)/shard_map/query_grad/pallas_call | solution.py:193
  460.3 12.1 %last.1 = (f32[768,768]{1,0:T(8,128)}, bf16[3,768,768]{2,1,0:T(8,128)(2,1)}, f32[8,768]{1,0:T(8,128)}) custom-call(bf16[768,768]{1,0:T(8,128)(2,1)} %tokens.3, f32[768,768]{1,0:T(8,128)} %get-tuple-element.62.grad_middle, bf16[768,768]{1,0:T(8,128)(2,1)} %query_grad.1.grad_query, bf16[768,768]{1,0:T(8,128)(2,1)} %get-tuple-element.71.grad_keys, ...), custom_call_target="tpu_custom_call" | custom-call | tf_op jit(solution)/shard_map/last/pallas_call | solution.py:470
  472.4 0.7 slice.60
  475.6 58.4 %scatter.1 = (f32[3,24,768]{2,1,0:T(8,128)}, f32[8,128]{1,0:T(8,128)}) custom-call(bf16[3,4,2,2,2,24,768]{6,5,4,3,2,1,0:T(8,128)(2,1)} %bitcast.51, f32[4,2,2,2,8,128]{5,4,3,2,1,0:T(8,128)} %bitcast.56), custom_call_target="tpu_custom_call" | custom-call | tf_op jit(solution)/shard_map/scatter/pallas_call | solution.py:836
  534.1 1.9 add_multiply_fusion.2
  536.1 0.7 slice.62
  537.6 1.0 add_multiply_fusion
  538.6 1.0 add_multiply_fusion.1
  539.7 0.7 add_multiply_fusion.3
  (89 shorter events, 13.4 us)
Async XLA Ops:
  205.2 37.1 %copy-start.12 = (f32[2,6,768]{2,1,0:T(8,128)S(1)}, f32[2,6,768]{2,1,0:T(8,128)}, u32[]{:S(2)}) copy-start(f32[2,6,768]{2,1,0:T(8,128)} %get-tuple-element.64.lse_ref) | copy-start | bytes 110596
  460.3 13.4 %copy-start.17 = (f32[1,3072]{1,0:T(1,128)S(1)}, f32[1,3072]{1,0:T(1,128)}, u32[]{:S(2)}) copy-start(f32[1,3072]{1,0:T(1,128)} %get-tuple-element.77) | copy-start | bytes 36868
  460.3 14.2 %copy-start.20 = (f32[8,768]{1,0:T(8,128)S(1)}, f32[8,768]{1,0:T(8,128)}, u32[]{:S(2)}) copy-start(f32[8,768]{1,0:T(8,128)} %get-tuple-element.76) | copy-start | bytes 73732
  474.6 59.5 %copy-start.2 = (f32[3,24,768]{2,1,0:T(8,128)S(1)}, f32[3,24,768]{2,1,0:T(8,128)}, u32[]{:S(2)}) copy-start(f32[3,24,768]{2,1,0:T(8,128)} %refs_0_.1) | copy-start | bytes 663556
  474.7 59.5 %copy-start.10 = (f32[3,24,768]{2,1,0:T(8,128)S(1)}, f32[3,24,768]{2,1,0:T(8,128)}, u32[]{:S(2)}) copy-start(f32[3,24,768]{2,1,0:T(8,128)} %param.28) | copy-start | bytes 663556
  474.7 59.5 %copy-start.11 = (f32[3,24,768]{2,1,0:T(8,128)S(1)}, f32[3,24,768]{2,1,0:T(8,128)}, u32[]{:S(2)}) copy-start(f32[3,24,768]{2,1,0:T(8,128)} %param.33) | copy-start | bytes 663556
  475.6 61.3 %copy-start.16 = (f32[12,24]{1,0:T(8,128)S(1)}, f32[12,24]{1,0:T(8,128)}, u32[]{:S(2)}) copy-start(f32[12,24]{1,0:T(8,128)} %param.27) | copy-start | bytes 3460
  475.6 61.3 %copy-start.18 = (f32[12,24]{1,0:T(8,128)S(1)}, f32[12,24]{1,0:T(8,128)}, u32[]{:S(2)}) copy-start(f32[12,24]{1,0:T(8,128)} %param.32) | copy-start | bytes 3460
  475.6 61.3 %copy-start.19 = (f32[12,24]{1,0:T(8,128)S(1)}, f32[12,24]{1,0:T(8,128)}, u32[]{:S(2)}) copy-start(f32[12,24]{1,0:T(8,128)} %param.37) | copy-start | bytes 3460
  475.6 62.0 %copy-start = (f32[96,768]{1,0:T(8,128)S(1)}, f32[96,768]{1,0:T(8,128)}, u32[]{:S(2)}) copy-start(f32[96,768]{1,0:T(8,128)} %refs_4_.1) | copy-start | bytes 884740
  475.6 62.0 %copy-start.4 = (f32[96,768]{1,0:T(8,128)S(1)}, f32[96,768]{1,0:T(8,128)}, u32[]{:S(2)}) copy-start(f32[96,768]{1,0:T(8,128)} %param.31) | copy-start | bytes 884740
  475.6 61.9 %copy-start.5 = (f32[96,768]{1,0:T(8,128)S(1)}, f32[96,768]{1,0:T(8,128)}, u32[]{:S(2)}) copy-start(f32[96,768]{1,0:T(8,128)} %param.36) | copy-start | bytes 884740
  475.6 61.9 %copy-start.9 = (f32[96,768]{1,0:T(8,128)S(1)}, f32[96,768]{1,0:T(8,128)}, u32[]{:S(2)}) copy-start(f32[96,768]{1,0:T(8,128)} %get-tuple-element.81) | copy-start | bytes 884740
  534.1 4.6 copy-start.1
  534.1 4.5 copy-start.6
  534.1 4.5 copy-start.7
  534.1 4.5 copy-start.8
  536.1 3.6 copy-start.3
  536.1 3.6 copy-start.13
  536.1 3.6 copy-start.14
  536.1 3.6 copy-start.15
